TPU v7x, 8 devices: a whole 2x2x1 slice. The times are simulated.
8 devices in a mesh: rep: 1 (over z), col: 2 (over y), row: 4 (over x, core).
Axes of the slice: x: 2, y: 2, z: 1, core: 2. Of those that a mesh axis runs over, the one named last changes fastest.
Arguments:
- part_mass: float32 [131072], P(('rep', 'col', 'row'))
- cell_idx: int32 [131072, 3], P(('rep', 'col', 'row'))
- cic_wts: float32 [131072, 3, 2], P(('rep', 'col', 'row'))
- live_mask: int32 [131072], P(('rep', 'col', 'row'))
- gas_mesh: float32 [192, 192, 192], P('rep', 'row', 'col')
Outputs:
- output 1: float32 [131072, 3], P(('rep', 'col', 'row'))
- output 2: float32 [1], P('rep')
All inputs are finite; a program needn't handle non-finite values.
Results may differ from a plain program's by a relative error of at most 0.001.
Values are sent between devices in bfloat16 or wider.
A program may use at most 1 GiB of HBM per device.

v0:
```python
import math
import jax
import jax.numpy as jnp
from jax import lax
from jax.sharding import PartitionSpec as P

MATMUL_PREC = lax.Precision.HIGHEST
GRAV_CONST = 1.0


def dft_table(out_ids, n_points, sign_val):
    in_ids = jnp.arange(n_points)
    phase_arg = ((out_ids[:, None] * in_ids[None, :]) % n_points).astype(jnp.float32) * (2.0 * math.pi / n_points)
    return jnp.cos(phase_arg), sign_val * jnp.sin(phase_arg)


def complex_matrix(out_ids, n_points, sign_val):
    cos_t, sin_t = dft_table(out_ids, n_points, sign_val)
    return jnp.stack([jnp.stack([cos_t, -sin_t]), jnp.stack([sin_t, cos_t])])


def wave_numbers(mode_ids, n_points):
    return ((mode_ids + n_points // 2) % n_points - n_points // 2).astype(jnp.float32)


def influence_of(norm_sq, n_points):
    k_unit = 2.0 * math.pi / n_points
    return jnp.where(norm_sq > 0, -4.0 * math.pi * GRAV_CONST / (k_unit * k_unit * jnp.maximum(norm_sq, 1.0)), 0.0)


def dft_apply(form, lhs_mat, rhs_arr):
    return jnp.einsum(form, lhs_mat, rhs_arr, precision=MATMUL_PREC, preferred_element_type=jnp.float32)


def local_stencil(cell_idx, cic_wts, grid_size, y_ext, z_ext):
    corner_off = jnp.arange(2)
    x_pts = (cell_idx[:, 0:1] + corner_off) % grid_size
    y_pts = cell_idx[:, 1:2] + corner_off
    z_pts = cell_idx[:, 2:3] + corner_off
    flat_pts = (x_pts[:, :, None, None] * y_ext + y_pts[:, None, :, None]) * z_ext + z_pts[:, None, None, :]
    stencil = cic_wts[:, 0, :, None, None] * cic_wts[:, 1, None, :, None] * cic_wts[:, 2, None, None, :]
    return flat_pts.reshape(-1), stencil.reshape(-1, 8)


def interpolate(ext_field, flat_pts, stencil, charge):
    samples = ext_field.reshape(-1, 3)[flat_pts].reshape(stencil.shape[0], 8, 3)
    grad_vals = jnp.sum(samples * stencil[:, :, None], axis=1)
    return -charge[:, None] * grad_vals


def solution(mesh):
    n_rows = mesh.shape["row"]
    n_cols = mesh.shape["col"]
    slot_axes = ("rep", "col", "row")
    to_next_row = [(k, (k + 1) % n_rows) for k in range(n_rows)]
    to_prev_row = [(k, (k - 1) % n_rows) for k in range(n_rows)]
    to_next_col = [(k, (k + 1) % n_cols) for k in range(n_cols)]
    to_prev_col = [(k, (k - 1) % n_cols) for k in range(n_cols)]

    def device_body(part_mass, cell_idx, cic_wts, live_mask, gas_block):
        grid_size, y_blk, z_blk = gas_block.shape
        per_dev = part_mass.shape[0]
        n_slots = per_dev * n_rows * n_cols
        row_id = lax.axis_index("row")
        col_id = lax.axis_index("col")
        flat_pts, stencil = local_stencil(cell_idx, cic_wts, grid_size, y_blk + 1, z_blk + 1)
        charge = part_mass * live_mask.astype(jnp.float32)
        spread = jax.ops.segment_sum((charge[:, None] * stencil).reshape(-1), flat_pts,
                                     num_segments=grid_size * (y_blk + 1) * (z_blk + 1))
        spread = spread.reshape(grid_size, y_blk + 1, z_blk + 1)
        from_row = lax.ppermute(spread[:, y_blk, :], "row", to_next_row)
        body_y = jnp.concatenate([spread[:, 0:1, :] + from_row[:, None, :], spread[:, 1:y_blk, :]], axis=1)
        from_col = lax.ppermute(body_y[:, :, z_blk], "col", to_next_col)
        density = jnp.concatenate([body_y[:, :, 0:1] + from_col[:, :, None], body_y[:, :, 1:z_blk]], axis=2) + gas_block

        full_ids = jnp.arange(grid_size)
        fwd_mat = complex_matrix(full_ids, grid_size, -1.0)
        stage_x = dft_apply("pkx,xyz->pkyz", fwd_mat[:, 0], density)
        swap_a = lax.all_to_all(stage_x, "row", 1, 2, tiled=True)
        stage_y = dft_apply("pqly,qkyz->plkz", fwd_mat, swap_a)
        swap_b = lax.all_to_all(stage_y, "col", 1, 3, tiled=True)
        rho_hat = dft_apply("pqmz,qlkz->pmlk", fwd_mat, swap_b)

        k_unit = 2.0 * math.pi / grid_size
        kz_n = wave_numbers(full_ids, grid_size)
        ky_n = wave_numbers(col_id * (grid_size // n_cols) + jnp.arange(grid_size // n_cols), grid_size)
        kx_n = wave_numbers(row_id * (grid_size // n_rows) + jnp.arange(grid_size // n_rows), grid_size)
        norm_sq = kz_n[:, None, None] ** 2 + ky_n[None, :, None] ** 2 + kx_n[None, None, :] ** 2
        influence = influence_of(norm_sq, grid_size)
        local_sum = jnp.sum(influence * (rho_hat[0] * rho_hat[0] + rho_hat[1] * rho_hat[1]))
        energy = lax.psum(local_sum, ("row", "col")) * (0.5 / (grid_size ** 3 * n_slots))
        i_pot = jnp.stack([-influence * rho_hat[1], influence * rho_hat[0]])
        deriv_hat = jnp.stack([i_pot * (k_unit * kx_n)[None, None, None, :],
                               i_pot * (k_unit * ky_n)[None, None, :, None],
                               i_pot * (k_unit * kz_n)[None, :, None, None]], axis=2)

        inv_mat = complex_matrix(full_ids, grid_size, 1.0)
        back_z = dft_apply("pqnm,qmclk->pnclk", inv_mat, deriv_hat)
        swap_c = lax.all_to_all(back_z, "col", 1, 3, tiled=True)
        back_y = dft_apply("pqyl,qzclk->pyzck", inv_mat, swap_c)
        swap_d = lax.all_to_all(back_y, "row", 1, 4, tiled=True)
        cos_t, sin_t = dft_table(full_ids, grid_size, 1.0)
        real_mat = jnp.stack([cos_t, -sin_t]) * (1.0 / grid_size ** 3)
        fields = dft_apply("qxk,qyzck->xyzc", real_mat, swap_d)

        from_row_next = lax.ppermute(fields[:, 0:1], "row", to_prev_row)
        ext_y = jnp.concatenate([fields, from_row_next], axis=1)
        from_col_next = lax.ppermute(ext_y[:, :, 0:1], "col", to_prev_col)
        ext_field = jnp.concatenate([ext_y, from_col_next], axis=2)
        part_force = interpolate(ext_field, flat_pts, stencil, charge)
        return part_force, energy.reshape(1)

    return jax.shard_map(
        device_body, mesh=mesh,
        in_specs=(P(slot_axes), P(slot_axes, None), P(slot_axes, None, None), P(slot_axes), P("rep", "row", "col")),
        out_specs=(P(slot_axes, None), P("rep")), check_vma=False)
```

profile of v0, /device:TPU:0, one launch (start us, length us, event | category | flops | bytes accessed | tf_op | source)
XLA Modules:
  0.0 3929.1 jit_solution(3170636537794817195)
XLA Ops:
  3.1 6.7 iota_add_fusion
  14.6 9.5 iota_add_fusion.1
  24.1 23.6 add_multiply_fusion
  47.7 40.3 %broadcast_add_fusion = s32[16384,2,2,2]{3,2,1,0:T(2,128)} fusion(s32[16384,2]{1,0:T(8,128)S(1)} %iota_add_fusion, s32[16384,2,2]{2,1,0:T(2,128)S(1)} %add_multiply_fusion), kind=kLoop, calls=%fused_computation.8 | loop fusion | flops 131072 | bytes 917504 | tf_op jit(solution)/shard_map/add | solution.py:40
  88.0 44.9 %reshape.494 = s32[131072]{0:T(1024)S(1)} reshape(s32[16384,2,2,2]{3,2,1,0:T(2,128)} %broadcast_add_fusion) | data formatting | bytes 1048576 | tf_op jit(solution)/shard_map/add | solution.py:40
  133.6 8.0 mul.402
  141.6 6.4 mul.403
  148.3 30.2 copy.77
  178.5 45.1 %mul.413 = f32[131072]{0:T(1024)S(1)} reshape(f32[16384,2,2,2]{3,2,1,0:T(2,128)} %copy.77) | data formatting | bytes 1048576 | tf_op jit(solution)/shard_map/mul | solution.py:41
  223.7 743.9 %scatter_custom_fusion = f32[912576]{0:T(1024)} fusion(s32[131072]{0:T(1024)S(1)} %reshape.494, f32[131072]{0:T(1024)S(1)} %mul.414, f32[]{:T(128)} %constant.52.clone.1), kind=kCustom, calls=%fused_computation.57 | custom fusion | flops 131072 | bytes 3650308 | tf_op jit(solution)/shard_map/scatter-add | solution.py:68
  967.6 8.9 reshape.480
  1005.6 12.0 fusion.24
  1017.6 9.4 fusion.25
  1027.1 5.7 copy.82
  1032.8 108.1 %all_to_all.72 = f32[2,192,48,96]{3,2,0,1:T(8,128)} all-to-all(f32[2,192,48,96]{3,2,0,1:T(8,128)S(1)} %copy.82), channel_id=1, replica_groups=mesh['rep'=1,'col'=2,'row'=4] {'row'}, dimensions={1} | all-to-all | bytes 14155776 | tf_op jit(solution)/shard_map/all_to_all | solution.py:79
  1145.9 17.5 convolution_bitcast_fusion.3
  1163.4 9.1 copy.85
  1172.5 7.5 all-to-all-start.1
  1180.4 103.0 %all-to-all-done.1 = f32[2,192,48,96]{3,2,0,1:T(8,128)} async-done(((f32[2,192,48,96]{3,2,0,1:T(8,128)}), f32[2,192,48,96]{3,2,0,1:T(8,128)}, u32[]{:S(2)}, u32[]{:S(2)}) %all-to-all-start.1) | async-done | bytes 7077920 | tf_op jit(solution)/shard_map/all_to_all | solution.py:81
  1283.4 17.2 copy.138
  1300.6 12.3 reshape.507
  1312.9 18.5 convolution_bitcast_fusion.2
  1335.1 10.5 fusion.12
  1345.6 51.3 %fusion.3 = f32[2,192,3,96,48]{3,1,4,2,0:T(8,128)S(1)} fusion(f32[2,192,1,96,48]{3,1,4,2,0:T(8,128)} %get-tuple-element.8, f32[2,192,1,96,48]{3,1,4,2,0:T(8,128)} %get-tuple-element.7, f32[2,192,1,96,48]{3,1,4,2,0:T(8,128)} %get-tuple-element.6, f32[2,2,192,192,1,1]{3,2,1,5,4,0:T(8,128)S(1)} %maximum_bitcast_fusion.8), kind=kOutput, calls=%fused_computation.12 | convolution fusion | flops 24471797760 | bytes 43057152 | tf_op jit(solution)/shard_map/pqnm,qmclk->pnclk/dot_general | solution.py:32
  1396.9 32.1 copy.89
  1429.0 12.8 all-to-all-start.2
  1441.7 66.5 %add.407 = s32[131072,1]{0,1:T(1,128)S(1)} reshape(s32[16384,2,2,2]{3,2,1,0:T(2,128)} %broadcast_add_fusion) | data formatting | bytes 1048576 | tf_op jit(solution)/shard_map/add | solution.py:40
  1508.3 238.3 %all-to-all-done.2 = f32[2,192,3,96,48]{3,4,2,0,1:T(8,128)} async-done(((f32[2,192,3,96,48]{3,4,2,0,1:T(8,128)}), f32[2,192,3,96,48]{3,4,2,0,1:T(8,128)}, u32[]{:S(2)}, u32[]{:S(2)}) %all-to-all-start.2) | async-done | bytes 21233696 | tf_op jit(solution)/shard_map/all_to_all | solution.py:99
  1746.6 47.1 %copy.137 = f32[2,2,96,3,96,48]{4,1,2,0,5,3:T(2,128)} copy(f32[2,2,96,3,96,48]{4,5,3,0,2,1:T(8,128)} %bitcast.41) | data formatting | bytes 42467328 | tf_op jit(solution)/shard_map/all_to_all | solution.py:99
  1793.7 33.5 reshape.512
  1827.2 50.2 %convolution_bitcast_fusion = f32[2,192,96,3,48]{2,1,4,3,0:T(8,128)S(1)} fusion(f32[2,96,3,192,48,1]{3,1,0,4,2,5:T(8,128)} %reshape.512, f32[2,2,192,192,1,1]{3,2,1,5,4,0:T(8,128)S(1)} %maximum_bitcast_fusion.9), kind=kOutput, calls=%fused_computation.13 | convolution fusion | flops 24461180928 | bytes 43057152 | tf_op jit(solution)/shard_map/pqyl,qzclk->pyzck/dot_general | solution.py:32
  1877.4 32.4 copy.91
  1909.9 8.9 all-to-all-start.3
  1919.3 305.7 %all-to-all-done.3 = f32[2,192,96,3,48]{2,4,3,0,1:T(8,128)} async-done(((f32[2,192,96,3,48]{2,4,3,0,1:T(8,128)}), f32[2,192,96,3,48]{2,4,3,0,1:T(8,128)}, u32[]{:S(2)}, u32[]{:S(2)}) %all-to-all-start.3) | async-done | bytes 21233696 | tf_op jit(solution)/shard_map/all_to_all | solution.py:101
  2225.1 21.4 copy.93
  2246.5 27.7 convolution_bitcast_fusion.1
  2283.5 13.0 pad_maximum_fusion.1
  2296.5 9.5 copy.95
  2306.3 5.4 fusion.28
  2317.0 23.5 psum.7
  2341.1 7.6 copy.96
  2348.8 14.9 pad_maximum_fusion.2
  2363.7 19.3 copy.139
  2382.9 18.7 reshape.520
  2401.6 14.3 reshape.521
  2415.9 1473.8 %gather_fusion = f32[131072,3]{0,1:T(4,128)S(1)} fusion(f32[912576,3]{0,1:T(4,128)} %bitcast.137, s32[131072]{0:T(1024)S(1)} %broadcast_clamp_fusion), kind=kCustom, calls=%fused_computation | custom fusion | bytes 3670016 | tf_op jit(solution)/shard_map/gather | solution.py:46
  3889.7 23.0 reshape.482
  3912.6 14.1 multiply_reduce_fusion
  (87 shorter events, 62.4 us)
Async XLA Ops:
  88.0 44.9 %copy-start.16 = (f32[16384]{0:T(1024)S(1)}, f32[16384]{0:T(1024)}, u32[]{:S(2)}) copy-start(f32[16384]{0:T(1024)} %param.5) | copy-start | bytes 196612
  88.0 44.9 %copy-start.17 = (s32[16384]{0:T(1024)S(1)}, s32[16384]{0:T(1024)}, u32[]{:S(2)}) copy-start(s32[16384]{0:T(1024)} %param.8) | copy-start | bytes 196612
  148.3 30.2 copy-start.5
  977.7 6.3 collective-permute-start
  979.3 16.4 copy-start.9
  980.1 15.6 copy-start.11
  983.2 2.6 copy-start.2
  993.2 4.5 collective-permute-start.1
  996.7 21.0 copy-start.3
  997.7 7.8 slice-start
  1000.7 4.9 slice-start.1
  1172.5 7.7 copy-start.7
  1172.5 7.7 copy-start.8
  1172.5 110.9 %all-to-all-start.1 = ((f32[2,192,48,96]{3,2,0,1:T(8,128)}), f32[2,192,48,96]{3,2,0,1:T(8,128)}, u32[]{:S(2)}, u32[]{:S(2)}) async-start(f32[2,192,48,96]{3,2,0,1:T(8,128)} %copy.85), calls=%async_computation.1 | async-start | bytes 18874368 | tf_op jit(solution)/shard_map/all_to_all | solution.py:81
  1180.1 151.3 %copy-start.18 = (f32[48]{0:T(128)}, f32[48]{0:T(128)S(1)}, u32[]{:S(2)}) copy-start(f32[48]{0:T(128)S(1)} %fusion.60) | copy-start | bytes 580
  1180.4 151.1 %copy-start.13 = (f32[192,96]{1,0:T(8,128)}, f32[192,96]{1,0:T(8,128)S(1)}, u32[]{:S(2)}) copy-start(f32[192,96]{1,0:T(8,128)S(1)} %broadcast_add_fusion.1) | copy-start | bytes 221188
  1300.6 12.3 copy-start.4
  1331.4 3.6 copy-start.1
  1429.0 317.6 %all-to-all-start.2 = ((f32[2,192,3,96,48]{3,4,2,0,1:T(8,128)}), f32[2,192,3,96,48]{3,4,2,0,1:T(8,128)}, u32[]{:S(2)}, u32[]{:S(2)}) async-start(f32[2,192,3,96,48]{3,4,2,0,1:T(8,128)} %copy.89), calls=%async_computation.2 | async-start | bytes 56623104 | tf_op jit(solution)/shard_map/all_to_all | solution.py:99
  1909.9 315.2 %all-to-all-start.3 = ((f32[2,192,96,3,48]{2,4,3,0,1:T(8,128)}), f32[2,192,96,3,48]{2,4,3,0,1:T(8,128)}, u32[]{:S(2)}, u32[]{:S(2)}) async-start(f32[2,192,96,3,48]{2,4,3,0,1:T(8,128)} %copy.91), calls=%async_computation.3 | async-start | bytes 56623104 | tf_op jit(solution)/shard_map/all_to_all | solution.py:101
  2225.1 21.4 copy-start.10
  2225.1 21.4 copy-start.12
  2246.5 32.8 copy-start.6
  2274.2 5.0 copy-start
  2279.2 4.3 collective-permute-start.2
  2296.5 9.8 copy-start.14
  2296.5 9.8 copy-start.19
  2306.0 35.1 collective-permute-start.3
  3912.6 14.1 copy-start.15
where the time goes:
time: 3970 us; the launch traced here: 3930 us
  local copies, waits for them, and re-layouts  2020 us (51%)
  other arithmetic  917 us (23%)
  waiting for transfers between devices  652 us (16%)
  matrix products  175 us (4%)
  blocking collectives  132 us (3%)
    gather x1, local copies, waits for them, and re-layouts, interpolate(): samples = ext_field.reshape(-1, 3)[flat_pts].reshape(stencil.shape[0], 8, 3)  1470 us
    scatter-add x1, other arithmetic, device_body(): jax.ops.segment_sum((charge[:, None] * stencil).reshape(-1), flat_pts, nu...  744 us
    all_to_all x1, waiting for transfers between devices, device_body(): swap_d = lax.all_to_all(back_y, 'row', 1, 4, tiled=True)  306 us
    all_to_all x1, waiting for transfers between devices, device_body(): swap_c = lax.all_to_all(back_z, 'col', 1, 3, tiled=True)  238 us
    dot_general x6, matrix products, dft_apply(): jnp.einsum(form, lhs_mat, rhs_arr, precision=MATMUL_PREC, preferred_eleme...  175 us
    add x2, local copies, waits for them, and re-layouts, local_stencil(): (x_pts[:, :, None, None] * y_ext + y_pts[:, None, :, None]) * z_ext  111 us
    all_to_all x1, blocking collectives, device_body(): swap_a = lax.all_to_all(stage_x, 'row', 1, 2, tiled=True)  108 us
    all_to_all x1, waiting for transfers between devices, device_body(): swap_b = lax.all_to_all(stage_y, 'col', 1, 3, tiled=True)  103 us
  transfers between devices with their start and end apart: 7, of which 5 were waited for; matrix products, arithmetic and copies ran while one was open for 2% of the time, Pallas kernels for 0%

commit v1 on v0

--- a/solution.py
+++ b/solution.py
@@ -1,11 +1,243 @@
+import functools
 import math
 import jax
 import jax.numpy as jnp
 from jax import lax
 from jax.sharding import PartitionSpec as P
+from jax.experimental import pallas as pl
+from jax.experimental.pallas import tpu as pltpu
 
 MATMUL_PREC = lax.Precision.HIGHEST
 GRAV_CONST = 1.0
+F32 = jnp.float32
+BF16 = jnp.bfloat16
+LANES = 128
+X_TILE = 96
+X_ROWS = 112
+Y_SHIFT = 15
+X_SHIFT = 7
+VMEM_BIG = 60 * 1024 * 1024
+
+
+def split3(val):
+    hi = val.astype(BF16)
+    rest = val - hi.astype(F32)
+    mid = rest.astype(BF16)
+    lo = (rest - mid.astype(F32)).astype(BF16)
+    return hi, mid, lo
+
+
+def bitonic(bufs):
+    sub = lax.broadcasted_iota(jnp.int32, (8, LANES), 0)
+    lane = lax.broadcasted_iota(jnp.int32, (8, LANES), 1)
+    base = lane * 128 + sub * 16
+
+    def bit(rank, pos):
+        return lax.shift_right_logical(rank, jnp.full_like(rank, pos)) & 1
+
+    def vreg_stage(k, j):
+        for v in range(16):
+            if v & (1 << j):
+                continue
+            low, high = pl.ds(8 * v, 8), pl.ds(8 * (v + (1 << j)), 8)
+            sgn = 1.0 - 2.0 * bit(base + v, k).astype(F32)
+            a = [b[low, :] for b in bufs]
+            c = [b[high, :] for b in bufs]
+            swap = a[0] * sgn > c[0] * sgn
+            for b, p, q in zip(bufs, a, c):
+                b[low, :] = jnp.where(swap, q, p)
+                b[high, :] = jnp.where(swap, p, q)
+
+    def roll_stage(k, j, dist, axis):
+        size = (8, LANES)[axis]
+        upper = bit(base, j)
+        keep_low = upper == 0
+        for v in range(16):
+            rows = pl.ds(8 * v, 8)
+            sgn = 1.0 - 2.0 * (bit(base + v, k) ^ upper).astype(F32)
+            own = [b[rows, :] for b in bufs]
+            other = [jnp.where(keep_low, pltpu.roll(o, size - dist, axis), pltpu.roll(o, dist, axis)) for o in own]
+            take = other[0] * sgn < own[0] * sgn
+            for b, o, p in zip(bufs, own, other):
+                b[rows, :] = jnp.where(take, p, o)
+
+    for k in range(1, 8):
+        for j in range(k - 1, -1, -1):
+            if j >= 4:
+                roll_stage(k, j, 1 << (j - 4), 0)
+            else:
+                vreg_stage(k, j)
+
+    def phase(k, carry):
+        def lane_stage(step, c):
+            j = k - 1 - step
+            roll_stage(k, j, jnp.left_shift(1, j - 7), 1)
+            return c
+        lax.fori_loop(0, k - 7, lane_stage, 0)
+        for j in (6, 5, 4):
+            roll_stage(k, j, 1 << (j - 4), 0)
+        for j in (3, 2, 1, 0):
+            vreg_stage(k, j)
+        return carry
+    lax.fori_loop(8, 15, phase, 0)
+
+
+def sort_kernel(n_arr, in_ref, out_ref, *bufs):
+    for n in range(n_arr):
+        bufs[n][...] = in_ref[n]
+    bitonic(bufs)
+    for n in range(n_arr):
+        out_ref[n] = bufs[n][...].T
+
+
+def sort_call(stacked):
+    n_arr = stacked.shape[0]
+    return pl.pallas_call(
+        functools.partial(sort_kernel, n_arr),
+        out_shape=jax.ShapeDtypeStruct(stacked.shape, F32),
+        in_specs=[pl.BlockSpec(memory_space=pltpu.VMEM)],
+        out_specs=pl.BlockSpec(memory_space=pltpu.VMEM),
+        scratch_shapes=[pltpu.VMEM((128, LANES), F32)] * n_arr,
+        name="slot_sort",
+    )(stacked)
+
+
+def pair_table(key, n_blk, n_xt):
+    b_ids = jnp.arange(n_blk + 1)
+    bounds = ((b_ids // n_xt) << Y_SHIFT) | (((b_ids % n_xt) * X_TILE) << X_SHIFT)
+    starts = jnp.sum((key[None, :] < bounds[:, None].astype(F32)).astype(jnp.int32), axis=1)
+    first, last = starts[:-1], starts[1:]
+    lo = first // LANES
+    count = jnp.where(last > first, (last + LANES - 1) // LANES - lo, 0)
+    ids = jnp.arange(n_blk)
+    ends = jnp.sum(jnp.where(ids[None, :] <= ids[:, None], count[None, :], 0), axis=1)
+    t_max = n_blk + 128
+    t_ids = jnp.arange(t_max)
+    blk = jnp.sum((ends[None, :] <= t_ids[:, None]).astype(jnp.int32), axis=1)
+    chunk = t_ids + jnp.sum(jnp.where(ids[None, :] == blk[:, None], (lo - ends + count)[None, :], 0), axis=1)
+    live = t_ids < ends[-1]
+    table = jnp.stack([jnp.where(live, blk, n_blk + 7), jnp.where(live, chunk, 0)])
+    return table.astype(jnp.int32), ends[-1:].astype(jnp.int32)
+
+
+def read_pair(t, table_ref, slot_ref, n_blk, n_xt):
+    blk = table_ref[0, t]
+    chunk = table_ref[1, t]
+    blk_in = jnp.minimum(blk, n_blk - 1)
+    y_pl = blk_in // n_xt
+    x_beg = pl.multiple_of((blk_in % n_xt) * X_TILE, 16)
+    code = slot_ref[0, pl.ds(chunk, 1), :].astype(jnp.int32)
+    x_c = (code >> X_SHIFT) & 255
+    b_c = (code >> Y_SHIFT) * n_xt
+    for m in range(1, n_xt):
+        b_c = b_c + (x_c >= m * X_TILE).astype(jnp.int32)
+    mask = b_c == blk
+    vals = [slot_ref[n, pl.ds(chunk, 1), :] for n in range(1, 5)]
+    return chunk, y_pl, x_beg, x_c - x_beg, code & 127, mask, vals
+
+
+def deposit_kernel(n_blk, n_xt, grid_size, table_ref, num_ref, slot_ref, rho_ref):
+    n_planes = rho_ref.shape[0]
+
+    def clear(y, c):
+        rho_ref[y] = jnp.zeros(rho_ref.shape[1:], F32)
+        return c
+    lax.fori_loop(0, n_planes, clear, 0)
+    row_x = lax.broadcasted_iota(jnp.int32, (X_ROWS, LANES), 0)
+    row_z = lax.broadcasted_iota(jnp.int32, (LANES, LANES), 0)
+
+    def one(t):
+        chunk, y_pl, x_beg, x_l, z_c, mask, (q, wx, wy, wz) = read_pair(t, table_ref, slot_ref, n_blk, n_xt)
+        q = jnp.where(mask, q, 0.0)
+        pick_x = jnp.concatenate([(row_x == x_l).astype(F32), (row_x == x_l + 1).astype(F32)], axis=1).astype(BF16)
+        on_z = jnp.where(row_z == z_c, 1.0 - wz, jnp.where(row_z == z_c + 1, wz, 0.0))
+        rows = []
+        for w_y in (1.0 - wy, wy):
+            rows.append(jnp.concatenate([on_z * (q * (1.0 - wx) * w_y), on_z * (q * wx * w_y)], axis=1))
+        parts = split3(jnp.concatenate(rows, axis=0))
+        res = None
+        for part in parts:
+            term = lax.dot_general(pick_x, part, (((1,), (1,)), ((), ())), preferred_element_type=F32)
+            res = term if res is None else res + term
+        for b in range(2):
+            rho_ref[y_pl + b, pl.ds(x_beg, X_ROWS), :] += res[:, b * LANES:(b + 1) * LANES]
+
+    def body(t, c):
+        one(2 * t)
+        one(2 * t + 1)
+        return c
+    lax.fori_loop(0, (num_ref[0] + 1) // 2, body, 0)
+
+    def wrap(y, c):
+        rho_ref[y, 0:8, :] += rho_ref[y, grid_size:grid_size + 8, :]
+        return c
+    lax.fori_loop(0, n_planes, wrap, 0)
+
+
+def interp_kernel(n_blk, n_xt, table_ref, num_ref, slot_ref, fhm_ref, flo_ref, out_ref):
+    out_ref[...] = jnp.zeros(out_ref.shape, F32)
+    row_x = lax.broadcasted_iota(jnp.int32, (X_ROWS, LANES), 0)
+    row_z = lax.broadcasted_iota(jnp.int32, (LANES, LANES), 0)
+
+    def one(t):
+        chunk, y_pl, x_beg, x_l, z_c, mask, (q, wx, wy, wz) = read_pair(t, table_ref, slot_ref, n_blk, n_xt)
+        pick_z = jnp.concatenate([(row_z == z_c).astype(F32), (row_z == z_c + 1).astype(F32)], axis=1).astype(BF16)
+        pick_2 = jnp.concatenate([pick_z, pick_z], axis=0)
+        on_x = jnp.where(row_x == x_l, 1.0 - wx, jnp.where(row_x == x_l + 1, wx, 0.0))
+        rows = pl.ds(x_beg, X_ROWS)
+        wt = [on_x * (1.0 - wy), on_x * wy]
+        for comp in range(3):
+            acc = None
+            for b in range(2):
+                got = jnp.dot(fhm_ref[y_pl + b, comp, rows, :], pick_2, preferred_element_type=F32)
+                got = got + jnp.dot(flo_ref[y_pl + b, comp, rows, :], pick_z, preferred_element_type=F32)
+                term = (got[:, :LANES] * (1.0 - wz) + got[:, LANES:] * wz) * wt[b]
+                acc = term if acc is None else acc + term
+            grad = jnp.sum(acc, axis=0, keepdims=True)
+            here = pl.ds(chunk, 1)
+            out_ref[comp, here, :] = jnp.where(mask, -q * grad, out_ref[comp, here, :])
+
+    def body(t, c):
+        one(2 * t)
+        one(2 * t + 1)
+        return c
+    lax.fori_loop(0, (num_ref[0] + 1) // 2, body, 0)
+
+
+SMEM_SPEC = pl.BlockSpec(memory_space=pltpu.SMEM)
+VMEM_SPEC = pl.BlockSpec(memory_space=pltpu.VMEM)
+
+
+def deposit_call(table, num, slots, y_ext, grid_size, n_blk, n_xt):
+    return pl.pallas_call(
+        functools.partial(deposit_kernel, n_blk, n_xt, grid_size),
+        out_shape=jax.ShapeDtypeStruct((y_ext, grid_size + 16, LANES), F32),
+        in_specs=[SMEM_SPEC, SMEM_SPEC, VMEM_SPEC], out_specs=VMEM_SPEC,
+        compiler_params=pltpu.CompilerParams(vmem_limit_bytes=VMEM_BIG), name="deposit",
+    )(table, num, slots)
+
+
+def interp_call(table, num, slots, fhm, flo, n_blk, n_xt):
+    return pl.pallas_call(
+        functools.partial(interp_kernel, n_blk, n_xt),
+        out_shape=jax.ShapeDtypeStruct((3, 128, LANES), F32),
+        in_specs=[SMEM_SPEC, SMEM_SPEC, VMEM_SPEC, VMEM_SPEC, VMEM_SPEC], out_specs=VMEM_SPEC,
+        compiler_params=pltpu.CompilerParams(vmem_limit_bytes=VMEM_BIG), name="interp",
+    )(table, num, slots, fhm, flo)
+
+
+def slot_arrays(part_mass, cell_idx, cic_wts, live_mask, y_blk):
+    charge = part_mass * live_mask.astype(F32)
+    code = (cell_idx[:, 1] << Y_SHIFT) | (cell_idx[:, 0] << X_SHIFT) | cell_idx[:, 2]
+    code = jnp.where(live_mask > 0, code, y_blk << Y_SHIFT).astype(F32)
+    upper = cic_wts[:, :, 1]
+    return jnp.stack([code, charge, upper[:, 0], upper[:, 1], upper[:, 2]]).reshape(5, 128, LANES)
+
+
+def home_ranks():
+    a = lax.broadcasted_iota(jnp.int32, (128, LANES), 0)
+    b = lax.broadcasted_iota(jnp.int32, (128, LANES), 1)
+    return (a * 128 + (b & 7) * 16 + (b >> 3)).astype(F32)
 
 
 def dft_table(out_ids, n_points, sign_val):
@@ -30,22 +262,6 @@
 
 def dft_apply(form, lhs_mat, rhs_arr):
     return jnp.einsum(form, lhs_mat, rhs_arr, precision=MATMUL_PREC, preferred_element_type=jnp.float32)
-
-
-def local_stencil(cell_idx, cic_wts, grid_size, y_ext, z_ext):
-    corner_off = jnp.arange(2)
-    x_pts = (cell_idx[:, 0:1] + corner_off) % grid_size
-    y_pts = cell_idx[:, 1:2] + corner_off
-    z_pts = cell_idx[:, 2:3] + corner_off
-    flat_pts = (x_pts[:, :, None, None] * y_ext + y_pts[:, None, :, None]) * z_ext + z_pts[:, None, None, :]
-    stencil = cic_wts[:, 0, :, None, None] * cic_wts[:, 1, None, :, None] * cic_wts[:, 2, None, None, :]
-    return flat_pts.reshape(-1), stencil.reshape(-1, 8)
-
-
-def interpolate(ext_field, flat_pts, stencil, charge):
-    samples = ext_field.reshape(-1, 3)[flat_pts].reshape(stencil.shape[0], 8, 3)
-    grad_vals = jnp.sum(samples * stencil[:, :, None], axis=1)
-    return -charge[:, None] * grad_vals
 
 
 def solution(mesh):
@@ -63,11 +279,13 @@
         n_slots = per_dev * n_rows * n_cols
         row_id = lax.axis_index("row")
         col_id = lax.axis_index("col")
-        flat_pts, stencil = local_stencil(cell_idx, cic_wts, grid_size, y_blk + 1, z_blk + 1)
-        charge = part_mass * live_mask.astype(jnp.float32)
-        spread = jax.ops.segment_sum((charge[:, None] * stencil).reshape(-1), flat_pts,
-                                     num_segments=grid_size * (y_blk + 1) * (z_blk + 1))
-        spread = spread.reshape(grid_size, y_blk + 1, z_blk + 1)
+        n_xt = grid_size // X_TILE
+        n_blk = y_blk * n_xt
+        raw = slot_arrays(part_mass, cell_idx, cic_wts, live_mask, y_blk)
+        table, num = pair_table(raw[0].reshape(-1), n_blk, n_xt)
+        slots = sort_call(jnp.concatenate([raw, home_ranks()[None]]))
+        rho = deposit_call(table, num, slots, y_blk + 1, grid_size, n_blk, n_xt)
+        spread = jnp.transpose(rho[:, :grid_size, :z_blk + 1], (1, 0, 2))
         from_row = lax.ppermute(spread[:, y_blk, :], "row", to_next_row)
         body_y = jnp.concatenate([spread[:, 0:1, :] + from_row[:, None, :], spread[:, 1:y_blk, :]], axis=1)
         from_col = lax.ppermute(body_y[:, :, z_blk], "col", to_next_col)
@@ -101,13 +319,20 @@
         swap_d = lax.all_to_all(back_y, "row", 1, 4, tiled=True)
         cos_t, sin_t = dft_table(full_ids, grid_size, 1.0)
         real_mat = jnp.stack([cos_t, -sin_t]) * (1.0 / grid_size ** 3)
-        fields = dft_apply("qxk,qyzck->xyzc", real_mat, swap_d)
-
-        from_row_next = lax.ppermute(fields[:, 0:1], "row", to_prev_row)
-        ext_y = jnp.concatenate([fields, from_row_next], axis=1)
-        from_col_next = lax.ppermute(ext_y[:, :, 0:1], "col", to_prev_col)
-        ext_field = jnp.concatenate([ext_y, from_col_next], axis=2)
-        part_force = interpolate(ext_field, flat_pts, stencil, charge)
+        fields = dft_apply("qxk,qyzck->ycxz", real_mat, swap_d)
+
+        from_row_next = lax.ppermute(fields[0:1], "row", to_prev_row)
+        ext_y = jnp.concatenate([fields, from_row_next], axis=0)
+        from_col_next = lax.ppermute(ext_y[..., 0:1], "col", to_prev_col)
+        ext = jnp.concatenate([ext_y, from_col_next, jnp.zeros(ext_y.shape[:3] + (LANES - z_blk - 1,), F32)], axis=3)
+        ext = jnp.concatenate([ext, ext[:, :, :16]], axis=2)
+        hi = lax.reduce_precision(ext, 8, 7)
+        mid = lax.reduce_precision(ext - hi, 8, 7)
+        low = ext - hi - mid
+        fhm = jnp.concatenate([hi, mid], axis=3).astype(BF16)
+        forces = interp_call(table, num, slots, fhm, low.astype(BF16), n_blk, n_xt)
+        back = sort_call(jnp.concatenate([slots[5:6], forces]))
+        part_force = back[1:4].reshape(3, per_dev).T
         return part_force, energy.reshape(1)
 
     return jax.shard_map(

time: 3970 us -> 1580 us (0.40)
  local copies, waits for them, and re-layouts: 2020 us -> 258 us
  other arithmetic: 917 us -> 93.1 us
  blocking collectives: 132 us -> 444 us
  waiting for transfers between devices: 652 us -> 416 us
  Pallas kernels: 0 us -> 150 us
    gather x1 -> x0, local copies, waits for them, and re-layouts: 1470 us -> none  [interpolate(): samples = ext_field.reshape(-1, 3)[flat_pts].reshape(stencil.shape[0], 8, 3)]
    scatter-add x1 -> x0, other arithmetic: 744 us -> none  [device_body(): jax.ops.segment_sum((charge[:, None] * stencil).reshape(-1), flat_pts, nu...]
    all_to_all x0 -> x1, blocking collectives: none -> 312 us  [device_body(): swap_d = lax.all_to_all(back_y, 'row', 1, 4, tiled=True)]
    all_to_all x1 -> x0, waiting for transfers between devices: 306 us -> none  [device_body(): swap_d = lax.all_to_all(back_y, 'row', 1, 4, tiled=True)]
    pallas_call x0 -> x4, Pallas kernels: none -> 150 us  [the longest x1 71.8 us: interp_call(): pl.pallas_call(functools.partial(interp_kernel, n_blk, n_xt), out_shape=j...]
    add x2 -> x0, local copies, waits for them, and re-layouts: 111 us -> none  [local_stencil(): (x_pts[:, :, None, None] * y_ext + y_pts[:, None, :, None]) * z_ext]
    mul x7 -> x0, local copies, waits for them, and re-layouts: 96.3 us -> none  [the longest x5 81.9 us: local_stencil(): cic_wts[:, 0, :, None, None] * cic_wts[:, 1, None, :, None]]
    add x4 -> x1, other arithmetic: 68.5 us -> 0.01 us  [pair_table(): lo - ends + count]
  transfers between devices with their start and end apart: 7 -> 6, of which waited for: 5 -> 5; matrix products, arithmetic and copies ran while one was open for 2% -> 1% of each run, Pallas kernels for 0% -> 0%
where the time goes in v1:
time: 1580 us; the launch traced here: 1570 us
  blocking collectives  444 us (28%)
  waiting for transfers between devices  416 us (26%)
  local copies, waits for them, and re-layouts  258 us (16%)
  matrix products  181 us (11%)
  Pallas kernels  150 us (9%)
  other arithmetic  93.1 us (6%)
  starting transfers between devices  20.3 us (1%)
    all_to_all x1, blocking collectives, device_body(): swap_d = lax.all_to_all(back_y, 'row', 1, 4, tiled=True)  312 us
    all_to_all x1, waiting for transfers between devices, device_body(): swap_c = lax.all_to_all(back_z, 'col', 1, 3, tiled=True)  305 us
    dot_general x6, matrix products, dft_apply(): jnp.einsum(form, lhs_mat, rhs_arr, precision=MATMUL_PREC, preferred_eleme...  181 us
    all_to_all x1, blocking collectives, device_body(): swap_a = lax.all_to_all(stage_x, 'row', 1, 2, tiled=True)  108 us
    all_to_all x1, waiting for transfers between devices, device_body(): swap_b = lax.all_to_all(stage_y, 'col', 1, 3, tiled=True)  103 us
    dot_general x5, local copies, waits for them, and re-layouts, dft_apply(): jnp.einsum(form, lhs_mat, rhs_arr, precision=MATMUL_PREC, preferred_eleme...  83.4 us
    all_to_all x2, local copies, waits for them, and re-layouts, device_body(): swap_c = lax.all_to_all(back_z, 'col', 1, 3, tiled=True)  80.6 us
    pallas_call x1, Pallas kernels, interp_call(): pl.pallas_call(functools.partial(interp_kernel, n_blk, n_xt), out_shape=j...  71.8 us
  transfers between devices with their start and end apart: 6, of which 5 were waited for; matrix products, arithmetic and copies ran while one was open for 1% of the time, Pallas kernels for 0%

profile of v1, /device:TPU:0, one launch (start us, length us, event | category | flops | bytes accessed | tf_op | source)
XLA Modules:
  0.0 1565.3 jit_solution(386829626550828571)
XLA Ops:
  0.7 1.4 slice_or_fusion
  4.9 1.2 slice.85
  8.2 12.3 slot_sort.2.slot_ref
  21.9 56.2 %deposit.1 = f32[49,208,128]{2,1,0:T(8,128)} custom-call(s32[2,224]{1,0:T(2,128)} %pad_add_fusion.table_ref, s32[1]{0:T(128)} %slice.92.num_ref, f32[6,128,128]{2,1,0:T(8,128)} %slot_sort.2.slot_ref), custom_call_target="tpu_custom_call" | custom-call | tf_op jit(solution)/shard_map/deposit/pallas_call | solution.py:212
  78.0 2.7 slice_bitcast_fusion
  85.1 2.9 fusion.17
  89.1 3.1 collective-permute-done.1
  92.1 3.1 copy.79
  95.3 4.7 fusion.19
  100.2 12.5 fusion.30
  112.7 5.9 copy.81
  118.6 108.1 %all_to_all.72 = f32[2,192,48,96]{3,2,0,1:T(8,128)} all-to-all(f32[2,192,48,96]{3,2,0,1:T(8,128)S(1)} %copy.81), channel_id=1, replica_groups=mesh['rep'=1,'col'=2,'row'=4] {'row'}, dimensions={1} | all-to-all | bytes 14155776 | tf_op jit(solution)/shard_map/all_to_all | solution.py:297
  226.7 5.1 copy.82
  231.8 17.2 %convolution_bitcast_fusion.2 = f32[2,192,48,96]{3,1,2,0:T(8,128)S(1)} fusion(f32[2,48,192,96,1]{3,2,0,1,4:T(8,128)S(1)} %bitcast.146, f32[1,2,192,192]{3,2,0,1:T(8,128)S(1)} %get-tuple-element.19, f32[1,2,192,192]{3,2,0,1:T(8,128)} %copy-done.2), kind=kOutput, calls=%fused_computation.61 | convolution fusion | flops 8153874432 | bytes 14745600 | tf_op jit(solution)/shard_map/pqly,qkyz->plkz/dot_general | solution.py:264
  249.0 9.1 copy.84
  258.1 7.4 all-to-all-start.1
  265.9 102.9 %all-to-all-done.1 = f32[2,192,48,96]{3,2,0,1:T(8,128)} async-done(((f32[2,192,48,96]{3,2,0,1:T(8,128)}), f32[2,192,48,96]{3,2,0,1:T(8,128)}, u32[]{:S(2)}, u32[]{:S(2)}) %all-to-all-start.1) | async-done | bytes 7077920 | tf_op jit(solution)/shard_map/all_to_all | solution.py:299
  368.8 17.3 %copy.146 = f32[2,2,96,48,96]{4,1,2,0,3:T(2,128)} copy(f32[2,2,96,48,96]{4,3,0,2,1:T(8,128)} %bitcast.33) | data formatting | bytes 14155776 | tf_op jit(solution)/shard_map/all_to_all | solution.py:299
  386.0 12.4 reshape.472
  398.4 18.5 %convolution_bitcast_fusion.1 = f32[2,192,96,48]{2,1,3,0:T(8,128)S(1)} fusion(f32[2,96,48,192,1]{3,1,0,2,4:T(8,128)} %reshape.472, f32[1,2,192,192]{3,2,0,1:T(8,128)S(1)} %get-tuple-element.19, f32[1,2,192,192]{3,2,0,1:T(8,128)S(1)} %copy-done.3), kind=kOutput, calls=%fused_computation.60 | convolution fusion | flops 8153874432 | bytes 14745600 | tf_op jit(solution)/shard_map/pqmz,qlkz->pmlk/dot_general | solution.py:264
  417.0 2.2 multiply_bitcast_fusion.1
  419.2 1.3 copy-done
  420.5 10.5 fusion.15
  431.0 51.6 %fusion.7 = f32[2,192,3,96,48]{3,1,4,2,0:T(8,128)S(1)} fusion(f32[2,192,1,96,48]{3,1,4,2,0:T(8,128)} %get-tuple-element.14, f32[2,192,1,96,48]{3,1,4,2,0:T(8,128)} %get-tuple-element.13, f32[2,192,1,96,48]{3,1,4,2,0:T(8,128)} %get-tuple-element.12, f32[2,2,192,192,1,1]{3,2,1,5,4,0:T(8,128)S(1)} %maximum_bitcast_fusion.8), kind=kOutput, calls=%fused_computation.19 | convolution fusion | flops 24471797760 | bytes 43057152 | tf_op jit(solution)/shard_map/pqnm,qmclk->pnclk/dot_general | solution.py:264
  482.6 32.1 %copy.88 = f32[2,192,3,96,48]{3,4,2,0,1:T(8,128)} copy(f32[2,192,3,96,48]{3,1,4,2,0:T(8,128)S(1)} %fusion.7) | data formatting | bytes 42467328 | tf_op jit(solution)/shard_map/pqnm,qmclk->pnclk/dot_general | solution.py:264
  514.7 12.5 all-to-all-start.2
  527.2 304.6 %all-to-all-done.2 = f32[2,192,3,96,48]{3,4,2,0,1:T(8,128)} async-done(((f32[2,192,3,96,48]{3,4,2,0,1:T(8,128)}), f32[2,192,3,96,48]{3,4,2,0,1:T(8,128)}, u32[]{:S(2)}, u32[]{:S(2)}) %all-to-all-start.2) | async-done | bytes 21233696 | tf_op jit(solution)/shard_map/all_to_all | solution.py:317
  831.8 47.1 %copy.144 = f32[2,2,96,3,96,48]{4,1,2,0,5,3:T(2,128)} copy(f32[2,2,96,3,96,48]{4,5,3,0,2,1:T(8,128)} %bitcast.42) | data formatting | bytes 42467328 | tf_op jit(solution)/shard_map/all_to_all | solution.py:317
  878.9 33.5 %reshape.477 = f32[2,96,3,192,48,1]{3,1,0,4,2,5:T(8,128)} reshape(f32[2,96,3,2,96,48]{4,3,1,0,5,2:T(2,128)} %bitcast.141) | data formatting | bytes 42467328 | tf_op jit(solution)/shard_map/all_to_all | solution.py:317
  912.4 50.5 %convolution_bitcast_fusion = f32[2,192,96,3,48]{2,1,4,3,0:T(8,128)} fusion(f32[2,96,3,192,48,1]{3,1,0,4,2,5:T(8,128)} %reshape.477, f32[2,2,192,192,1,1]{3,2,1,5,4,0:T(8,128)S(1)} %maximum_bitcast_fusion.9), kind=kOutput, calls=%fused_computation.20 | convolution fusion | flops 24461180928 | bytes 43057152 | tf_op jit(solution)/shard_map/pqyl,qzclk->pyzck/dot_general | solution.py:264
  962.8 24.4 %copy.90 = f32[2,192,96,3,48]{2,4,3,0,1:T(8,128)S(1)} copy(f32[2,192,96,3,48]{2,1,4,3,0:T(8,128)} %convolution_bitcast_fusion) | data formatting | bytes 42467328 | tf_op jit(solution)/shard_map/pqyl,qzclk->pyzck/dot_general | solution.py:264
  987.2 311.9 %all_to_all.73 = f32[2,192,96,3,48]{2,4,3,0,1:T(8,128)} all-to-all(f32[2,192,96,3,48]{2,4,3,0,1:T(8,128)S(1)} %copy.90), channel_id=1, replica_groups=mesh['rep'=1,'col'=2,'row'=4] {'row'}, dimensions={1} | all-to-all | bytes 42467328 | tf_op jit(solution)/shard_map/all_to_all | solution.py:319
  1299.2 21.4 %copy.92 = f32[2,48,96,3,4,48]{2,5,4,3,1,0:T(8,128)} copy(f32[2,48,96,3,4,48]{2,5,3,0,1,4:T(8,128)} %bitcast.142) | data formatting | bytes 42467328 | tf_op jit(solution)/shard_map/all_to_all | solution.py:319
  1320.5 31.1 %fusion.10 = f32[48,96,3,192]{1,3,0,2:T(8,128)} fusion(f32[2,48,96,3,192]{2,4,3,1,0:T(8,128)} %bitcast.143, f32[1,192,192]{2,1,0:T(8,128)S(1)} %copy-done.9, f32[1,192,192]{2,1,0:T(8,128)S(1)} %copy-done.7), kind=kOutput, calls=%fused_computation.23 | convolution fusion | flops 12230737920 | bytes 32145408 | tf_op jit(solution)/shard_map/qxk,qyzck->ycxz/dot_general | solution.py:264
  1351.6 12.0 copy.145
  1364.7 4.2 collective-permute-done.2
  1368.9 13.0 pad_maximum_fusion.5
  1381.9 9.5 copy.95
  1391.7 5.4 fusion.37
  1397.1 23.5 %psum.7 = f32[]{:T(128)} all-reduce(f32[]{:T(128)} %fusion.37), channel_id=1, replica_groups=mesh['rep'=1,'col'=2,'row'=4] {'row','col'}, use_global_device_ids=true, to_apply=%region_5.6 | all-reduce | flops 1 | bytes 8 | tf_op jit(solution)/shard_map/psum | solution.py:309
  1421.3 7.7 copy.96
  1429.0 6.9 broadcast_in_dim.79
  1436.0 29.5 %fusion.5 = (bf16[49,3,208,128]{3,2,1,0:T(8,128)(2,1)}, f32[49,3,208,128]{3,2,1,0:T(8,128)}) fusion(f32[49,3,192,31]{3,2,1,0:T(8,128)} %broadcast_in_dim.79, f32[49,3,192,1]{3,2,1,0:T(8,128)} %copy.96, f32[1,3,192,96]{3,2,1,0:T(8,128)S(1)} %collective-permute-done.2, f32[48,3,192,96]{3,2,1,0:T(8,128)} %bitcast.140), kind=kLoop, calls=%fused_computation.11 | loop fusion | flops 46964736 | bytes 37933056 | tf_op jit(solution)/shard_map/convert_element_type | solution.py:333
  1465.4 7.0 reduce-precision_convert_fusion.1
  1472.4 6.5 pad_maximum_fusion.4.fhm_ref
  1479.0 71.8 %interp.1 = f32[3,128,128]{2,1,0:T(8,128)} custom-call(s32[2,224]{1,0:T(2,128)} %pad_add_fusion.table_ref, s32[1]{0:T(128)} %slice.92.num_ref, f32[6,128,128]{2,1,0:T(8,128)} %slot_sort.2.slot_ref, bf16[49,3,208,256]{3,2,1,0:T(8,128)(2,1)} %pad_maximum_fusion.4.fhm_ref, bf16[49,3,208,128]{3,2,1,0:T(8,128)(2,1)} %get-tuple-element.2.flo_ref), custom_call_target="tpu_custom_call" | custom-call | tf_op jit(solution)/shard_map/interp/pallas_call | solution.py:221
  1550.8 1.6 pad_maximum_fusion.13.in_ref
  1552.4 9.5 slot_sort.3
  (80 shorter events, 15.2 us)
Async XLA Ops:
  7.5 0.8 copy-start.12
  80.7 4.1 collective-permute-start
  81.6 13.7 copy-start.6
  82.4 12.9 copy-start.8
  82.9 2.2 copy-start.1
  88.0 4.1 collective-permute-start.1
  89.1 11.0 copy-start.2
  92.1 7.9 slice-start
  95.3 4.9 slice-start.1
  258.1 7.6 copy-start.4
  258.1 7.6 copy-start.5
  258.1 110.6 %all-to-all-start.1 = ((f32[2,192,48,96]{3,2,0,1:T(8,128)}), f32[2,192,48,96]{3,2,0,1:T(8,128)}, u32[]{:S(2)}, u32[]{:S(2)}) async-start(f32[2,192,48,96]{3,2,0,1:T(8,128)} %copy.84), calls=%async_computation.1 | async-start | bytes 18874368 | tf_op jit(solution)/shard_map/all_to_all | solution.py:299
  265.6 151.3 %copy-start.13 = (f32[48]{0:T(128)}, f32[48]{0:T(128)S(1)}, u32[]{:S(2)}) copy-start(f32[48]{0:T(128)S(1)} %fusion.76) | copy-start | bytes 580
  265.9 151.1 %copy-start.10 = (f32[192,96]{1,0:T(8,128)}, f32[192,96]{1,0:T(8,128)S(1)}, u32[]{:S(2)}) copy-start(f32[192,96]{1,0:T(8,128)S(1)} %broadcast_add_fusion) | copy-start | bytes 221188
  386.0 12.4 copy-start.3
  416.9 3.5 copy-start
  514.7 317.1 %all-to-all-start.2 = ((f32[2,192,3,96,48]{3,4,2,0,1:T(8,128)}), f32[2,192,3,96,48]{3,4,2,0,1:T(8,128)}, u32[]{:S(2)}, u32[]{:S(2)}) async-start(f32[2,192,3,96,48]{3,4,2,0,1:T(8,128)} %copy.88), calls=%async_computation.2 | async-start | bytes 56623104 | tf_op jit(solution)/shard_map/all_to_all | solution.py:317
  1299.2 21.4 %copy-start.7 = (f32[1,192,192]{2,1,0:T(8,128)S(1)}, f32[1,192,192]{2,1,0:T(8,128)}, u32[]{:S(2)}) copy-start(f32[1,192,192]{2,1,0:T(8,128)} %copy-done.6) | copy-start | bytes 442372
  1299.2 21.4 %copy-start.9 = (f32[1,192,192]{2,1,0:T(8,128)S(1)}, f32[1,192,192]{2,1,0:T(8,128)}, u32[]{:S(2)}) copy-start(f32[1,192,192]{2,1,0:T(8,128)} %copy-done.8) | copy-start | bytes 442372
  1364.6 4.3 collective-permute-start.2
  1381.9 9.8 copy-start.11
  1381.9 9.8 copy-start.14
  1391.4 29.9 %collective-permute-start.3 = (f32[49,3,192,1]{2,3,1,0:T(1,128)S(1)}, f32[49,3,192,1]{2,3,1,0:T(1,128)S(1)}, u32[]{:S(2)}, u32[]{:S(2)}) collective-permute-start(f32[49,3,192,1]{2,3,1,0:T(1,128)S(1)} %copy.95), channel_id=1, source_target_pairs={{0,4},{4,0},{1,5},{5,1},{2,6},{6,2},{3,7},{7,3}} | collective-permute-start | bytes 338696 | tf_op jit(solution)/shard_map/ppermute | solution.py:326
  1479.0 71.8 %slice-start.2 = ((f32[6,128,128]{2,1,0:T(8,128)}), f32[1,128,128]{2,1,0:T(8,128)S(1)}, s32[]{:S(2)}) async-start(f32[6,128,128]{2,1,0:T(8,128)} %slot_sort.2.slot_ref), calls=%async_computation.6 | async-start | bytes 131072 | tf_op jit(solution)/shard_map/slice | solution.py:334

commit v2 on v1

--- a/solution.py
+++ b/solution.py
@@ -1,5 +1,6 @@
 import functools
 import math
+import numpy as np
 import jax
 import jax.numpy as jnp
 from jax import lax
@@ -240,102 +241,388 @@
     return (a * 128 + (b & 7) * 16 + (b >> 3)).astype(F32)
 
 
-def dft_table(out_ids, n_points, sign_val):
-    in_ids = jnp.arange(n_points)
-    phase_arg = ((out_ids[:, None] * in_ids[None, :]) % n_points).astype(jnp.float32) * (2.0 * math.pi / n_points)
-    return jnp.cos(phase_arg), sign_val * jnp.sin(phase_arg)
-
-
-def complex_matrix(out_ids, n_points, sign_val):
-    cos_t, sin_t = dft_table(out_ids, n_points, sign_val)
-    return jnp.stack([jnp.stack([cos_t, -sin_t]), jnp.stack([sin_t, cos_t])])
-
-
-def wave_numbers(mode_ids, n_points):
-    return ((mode_ids + n_points // 2) % n_points - n_points // 2).astype(jnp.float32)
-
-
-def influence_of(norm_sq, n_points):
-    k_unit = 2.0 * math.pi / n_points
-    return jnp.where(norm_sq > 0, -4.0 * math.pi * GRAV_CONST / (k_unit * k_unit * jnp.maximum(norm_sq, 1.0)), 0.0)
-
-
-def dft_apply(form, lhs_mat, rhs_arr):
-    return jnp.einsum(form, lhs_mat, rhs_arr, precision=MATMUL_PREC, preferred_element_type=jnp.float32)
+def mul6(a, b):
+    res = None
+    for m, n in ((2, 0), (0, 2), (1, 1), (1, 0), (0, 1), (0, 0)):
+        term = jnp.dot(a[m], b[n], preferred_element_type=F32)
+        res = term if res is None else res + term
+    return res
+
+
+def table3(mat):
+    mat = mat.astype(np.float32)
+    hi = mat.astype(BF16)
+    mid = (mat - hi.astype(np.float32)).astype(BF16)
+    lo = (mat - hi.astype(np.float32) - mid.astype(np.float32)).astype(BF16)
+    return np.stack([hi, mid, lo])
+
+
+class Plan:
+    def __init__(self, n, n_chip, y_blk, z_blk):
+        self.n, self.n_chip, self.y_blk, self.z_blk = n, n_chip, y_blk, z_blk
+        self.y_ext = y_blk + 1
+        self.z_ext = z_blk + 1
+        self.y_pad = -(-self.y_ext // 8) * 8
+        self.half_k = n // 2 + 1
+        self.slots = -(-self.half_k // (2 * n_chip))
+        self.per_core = self.slots * n_chip
+        self.k_pad = -(-self.per_core // 8) * 8
+        self.rows = -(-(self.slots * self.y_ext + 1) // 8) * 8
+        self.y_even = self.y_ext + self.y_ext % 2
+        self.x_pad = n + 16
+
+    def angle(self, k, r):
+        return 2.0 * np.pi / self.n * ((k[:, None] * r[None, :]) % self.n)
+
+    def lane_order(self):
+        kz = np.concatenate([np.arange(128), np.arange(128), np.arange(128, self.n), np.arange(128, self.n)])
+        im = np.concatenate([np.zeros(128), np.ones(128), np.zeros(self.n - 128), np.ones(self.n - 128)]) > 0
+        return kz, im
+
+    def deriv(self, k):
+        sgn = np.where(k < self.n // 2, k, k - self.n)
+        return np.where(k == self.n // 2, 0, sgn) * (2.0 * np.pi / self.n)
+
+    def tables(self):
+        n = self.n
+        out = {}
+        mx = np.zeros((2, 2, self.k_pad, n))
+        mi = np.zeros((2, 2, self.x_pad, 2, self.k_pad))
+        for h in range(2):
+            kx = h * self.per_core + np.arange(self.per_core)
+            ok = (kx < self.half_k)[:, None]
+            th = self.angle(kx, np.arange(n))
+            mx[h, 0, :self.per_core] = np.where(ok, np.cos(th), 0.0)
+            mx[h, 1, :self.per_core] = np.where(ok, -np.sin(th), 0.0)
+            th = self.angle(kx, np.arange(self.x_pad))
+            wt = np.where(kx < self.half_k, np.where((kx == 0) | (kx == n // 2), 1.0, 2.0), 0.0) / float(n) ** 3
+            kd = np.where(kx < n // 2, kx, 0) * (2.0 * np.pi / n) * wt
+            mi[h, 0, :, 0, :self.per_core] = (-kd[:, None] * np.sin(th)).T
+            mi[h, 0, :, 1, :self.per_core] = (-kd[:, None] * np.cos(th)).T
+            mi[h, 1, :, 0, :self.per_core] = (wt[:, None] * np.cos(th)).T
+            mi[h, 1, :, 1, :self.per_core] = (-wt[:, None] * np.sin(th)).T
+        out["mx"] = table3(mx.reshape(2, 2 * self.k_pad, n))
+        out["mi"] = table3(mi.reshape(2, 2, self.x_pad, 2 * self.k_pad))
+        kz, im = self.lane_order()
+        wz = np.zeros((2, 2, LANES, 2 * n))
+        wi = np.zeros((2, 2 * n, 4, LANES))
+        kd = self.deriv(kz)[:, None]
+        for h in range(2):
+            z = (h * self.z_blk + np.arange(self.z_ext)) % n
+            c, s = np.cos(self.angle(kz, z)), np.sin(self.angle(kz, z))
+            wz[h, 0, :self.z_ext] = np.where(im[:, None], -s, c).T
+            wz[h, 1, :self.z_ext] = np.where(im[:, None], c, s).T
+            re_w, im_w = np.where(im[:, None], -s, c), np.where(im[:, None], c, s)
+            wi[h, :, 0, :self.z_ext] = re_w
+            wi[h, :, 1, :self.z_ext] = im_w
+            wi[h, :, 2, :self.z_ext] = -kd * im_w
+            wi[h, :, 3, :self.z_ext] = kd * re_w
+        out["wz"] = table3(wz)
+        out["wi"] = table3(wi.reshape(2, 2 * n, 4 * LANES))
+        ky = np.arange(n)
+        my = np.zeros((2, n, self.n_chip, self.y_pad))
+        ei = np.zeros((self.n_chip, 4, self.y_pad, n))
+        for i in range(self.n_chip):
+            y = (i * self.y_blk + np.arange(self.y_ext)) % n
+            th = self.angle(ky, y)
+            my[0, :, i, :self.y_ext] = np.cos(th)
+            my[1, :, i, :self.y_ext] = np.sin(th)
+            ei[i, 0, :self.y_ext] = np.cos(th).T
+            ei[i, 1, :self.y_ext] = np.sin(th).T
+            ei[i, 2, :self.y_ext] = (self.deriv(ky)[:, None] * np.cos(th)).T
+            ei[i, 3, :self.y_ext] = (self.deriv(ky)[:, None] * np.sin(th)).T
+        out["my"] = table3(my.reshape(2 * n, self.n_chip * self.y_pad))
+        out["ei"] = table3(ei.reshape(self.n_chip, 4 * self.y_pad, n))
+        return out
+
+
+def x_kernel(plan, core_ref, rho_ref, gas_ref, mx_ref, own_ref, send_ref, tmp_ref):
+    step = pl.program_id(0)
+    core = core_ref[0]
+    n, kp = plan.n, plan.k_pad
+
+    @pl.when(step == 0)
+    def _():
+        tmp_ref[...] = jnp.zeros(tmp_ref.shape, F32)
+
+    live = (2 * step < plan.y_blk).astype(F32)
+    tmp_ref[:, :, :plan.z_blk] = gas_ref[...] * live
+    data = jnp.concatenate([rho_ref[y, :n, :] + tmp_ref[y] for y in range(2)], axis=1)
+    parts = split3(data)
+    for half, out in ((core, own_ref), (1 - core, send_ref)):
+        res = mul6([mx_ref[m, half] for m in range(3)], parts)
+        for y in range(2):
+            for ri in range(2):
+                out[ri, y] = res[ri * kp:(ri + 1) * kp, y * LANES:(y + 1) * LANES]
+
+
+def x_call(plan, core, rho, gas, mx):
+    steps = plan.y_even // 2
+    last = plan.y_blk // 2 - 1
+    shape = jax.ShapeDtypeStruct((2, plan.y_even, plan.k_pad, LANES), F32)
+    out_spec = pl.BlockSpec((2, 2, plan.k_pad, LANES), lambda i: (0, i, 0, 0))
+    return pl.pallas_call(
+        functools.partial(x_kernel, plan), grid=(steps,), out_shape=(shape, shape),
+        in_specs=[SMEM_SPEC, pl.BlockSpec((2, plan.x_pad, LANES), lambda i: (i, 0, 0)),
+                  pl.BlockSpec((2, plan.n, plan.z_blk), lambda i: (jnp.minimum(i, last), 0, 0)),
+                  pl.BlockSpec(mx.shape, lambda i: (0, 0, 0, 0))],
+        out_specs=(out_spec, out_spec),
+        scratch_shapes=[pltpu.VMEM((2, plan.n, LANES), F32)], name="dft_x",
+    )(core, rho, gas, mx)
+
+
+Z_BATCH = 5
+
+
+def z_kernel(plan, core_ref, own_ref, rec_ref, wz_ref, out_ref):
+    step = pl.program_id(0)
+    core = core_ref[0]
+    kp, sl, ye = plan.k_pad, plan.slots, plan.y_ext
+
+    @pl.when(step == 0)
+    def _():
+        for t in range(plan.n_chip):
+            for g in range(3):
+                out_ref[t, g, plan.rows - 8:plan.rows, :] = jnp.zeros((8, LANES), F32)
+
+    flat = (Z_BATCH * kp, LANES)
+    data = jnp.concatenate([own_ref[0].reshape(flat), rec_ref[0].reshape(flat),
+                            own_ref[1].reshape(flat), rec_ref[1].reshape(flat)], axis=1)
+    wts = [jnp.concatenate([wz_ref[m, core, 0], wz_ref[m, 1 - core, 0], wz_ref[m, core, 1], wz_ref[m, 1 - core, 1]], axis=0)
+           for m in range(3)]
+    res = mul6(split3(data), wts)
+    for b in range(Z_BATCH):
+        y = step * Z_BATCH + b
+
+        @pl.when(y < ye)
+        def _():
+            for t in range(plan.n_chip):
+                for g in range(3):
+                    r0 = b * kp + t * sl
+                    out_ref[t, g, pl.ds(y, sl, stride=ye), :] = res[r0:r0 + sl, g * LANES:(g + 1) * LANES]
+
+
+def z_call(plan, core, own, rec, wz):
+    blk = pl.BlockSpec((2, Z_BATCH, plan.k_pad, LANES), lambda i: (0, i, 0, 0))
+    shape = (plan.n_chip, 3, plan.rows, LANES)
+    return pl.pallas_call(
+        functools.partial(z_kernel, plan), grid=(plan.y_even // Z_BATCH,),
+        out_shape=jax.ShapeDtypeStruct(shape, F32),
+        in_specs=[SMEM_SPEC, blk, blk, pl.BlockSpec(wz.shape, lambda i: (0,) * 5)],
+        out_specs=pl.BlockSpec(shape, lambda i: (0, 0, 0, 0)),
+        compiler_params=pltpu.CompilerParams(vmem_limit_bytes=VMEM_BIG), name="dft_z",
+    )(core, own, rec, wz)
+
+
+def signed(ids, n):
+    return jnp.where(ids < n // 2, ids, ids - n).astype(F32)
+
+
+def y_kernel(plan, base_ref, rec_ref, my_ref, ei_ref, out_ref, buf_ref):
+    n, ye, yp = plan.n, plan.y_ext, plan.y_pad
+    k_unit = 2.0 * math.pi / n
+    buf_ref[...] = jnp.zeros(buf_ref.shape, F32)
+    tail = slice(plan.rows - 8, plan.rows)
+    for i in range(plan.n_chip):
+        for c in range(2):
+            for g in range(3):
+                out_ref[i, c, g, tail, :] = jnp.zeros((8, LANES), F32)
+    lane = lax.broadcasted_iota(jnp.int32, (n, LANES), 1)
+    ky = signed(lax.broadcasted_iota(jnp.int32, (n, LANES), 0), n)
+    kz_a = signed(lane, n)
+    kz_b = signed(128 + (lane & 63), n)
+    yz_a, yz_b = ky * ky + kz_a * kz_a, ky * ky + kz_b * kz_b
+    flip = jnp.where(lax.broadcasted_iota(jnp.int32, (1, LANES), 1) < 64, 1.0, -1.0)
+
+    def slot(s, energy):
+        rows = pl.ds(s * ye, ye)
+        for i in range(plan.n_chip):
+            for g in range(3):
+                buf_ref[g, i * yp:i * yp + ye, :] = rec_ref[i, g, rows, :]
+        data = jnp.concatenate([buf_ref[g] for g in range(3)], axis=1)
+        q = mul6([my_ref[m] for m in range(3)], split3(data))
+        c = [q[:n, g * LANES:(g + 1) * LANES] for g in range(3)]
+        d = [q[n:, g * LANES:(g + 1) * LANES] for g in range(3)]
+        r0 = c[0] + d[1]
+        r1 = c[1] - d[0]
+        r2 = c[2] + flip * pltpu.roll(d[2], 64, 1)
+        kx_i = base_ref[0] + s
+        kx = kx_i.astype(F32)
+        weight = jnp.where(kx_i < n // 2, jnp.where(kx_i == 0, 1.0, 2.0), jnp.where(kx_i == n // 2, 1.0, 0.0))
+        scale = -4.0 * math.pi * GRAV_CONST / (k_unit * k_unit)
+
+        def influence(yz):
+            sq = yz + kx * kx
+            return jnp.where(sq > 0, scale / jnp.maximum(sq, 1.0), 0.0)
+        g_a, g_b = influence(yz_a), influence(yz_b)
+        power = g_a * (r0 * r0 + r1 * r1) + g_b * (r2 * r2)
+        energy = energy + weight * jnp.sum(power, axis=0, keepdims=True)
+        parts = split3(jnp.concatenate([g_a * r0, g_a * r1, g_b * r2], axis=1))
+        for i in range(plan.n_chip):
+            p = mul6([ei_ref[m, i] for m in range(3)], parts)
+            blk = [[p[u * yp:(u + 1) * yp, g * LANES:(g + 1) * LANES] for g in range(3)] for u in range(4)]
+            co, si, ck, sk = blk
+            pot = (co[0] - si[1], co[1] + si[0], co[2] - flip * pltpu.roll(si[2], 64, 1))
+            dy = (-(ck[1] + sk[0]), ck[0] - sk[1], -flip * pltpu.roll(ck[2], 64, 1) - sk[2])
+            for comp, val in ((0, pot), (1, dy)):
+                for g in range(3):
+                    out_ref[i, comp, g, rows, :] = val[g][:ye]
+        return energy
+
+    energy = lax.fori_loop(0, plan.slots, slot, jnp.zeros((1, LANES), F32))
+    e_row = plan.slots * ye
+    for i in range(plan.n_chip):
+        out_ref[i, 0, 0, e_row:e_row + 1, :] = energy
+
+
+def y_call(plan, base, rec, my, ei):
+    return pl.pallas_call(
+        functools.partial(y_kernel, plan),
+        out_shape=jax.ShapeDtypeStruct((plan.n_chip, 2, 3, plan.rows, LANES), F32),
+        in_specs=[SMEM_SPEC, VMEM_SPEC, VMEM_SPEC, VMEM_SPEC], out_specs=VMEM_SPEC,
+        scratch_shapes=[pltpu.VMEM((3, plan.n_chip * plan.y_pad, LANES), F32)],
+        compiler_params=pltpu.CompilerParams(vmem_limit_bytes=VMEM_BIG), name="dft_y",
+    )(base, rec, my, ei)
+
+
+def zi_kernel(plan, core_ref, rec_ref, wi_ref, own_ref, send_ref, buf_ref):
+    step = pl.program_id(0)
+    core = core_ref[0]
+    kp, sl, ye = plan.k_pad, plan.slots, plan.y_ext
+
+    @pl.when(step == 0)
+    def _():
+        buf_ref[...] = jnp.zeros(buf_ref.shape, F32)
+
+    for comp in range(2):
+        for b in range(Z_BATCH):
+            for t in range(plan.n_chip):
+                for g in range(3):
+                    buf_ref[comp, b, t * sl:(t + 1) * sl, g * LANES:(g + 1) * LANES] = (
+                        rec_ref[t, comp, g, pl.ds(step * Z_BATCH + b, sl, stride=ye), :])
+    half_rows = Z_BATCH * kp
+    parts = split3(buf_ref[...].reshape(2 * half_rows, 2 * plan.n))
+    pot = [p[:half_rows] for p in parts]
+    for half, out in ((core, own_ref), (1 - core, send_ref)):
+        plain = mul6(parts, [wi_ref[m, half, :, :2 * LANES] for m in range(3)])
+        along = mul6(pot, [wi_ref[m, half, :, 2 * LANES:] for m in range(3)])
+        for b in range(Z_BATCH):
+            for ri in range(2):
+                ln = slice(ri * LANES, (ri + 1) * LANES)
+                out[0, ri, b] = plain[b * kp:(b + 1) * kp, ln]
+                out[1, ri, b] = plain[half_rows + b * kp:half_rows + (b + 1) * kp, ln]
+                out[2, ri, b] = along[b * kp:(b + 1) * kp, ln]
+
+    @pl.when(step == pl.num_programs(0) - 1)
+    def _():
+        e_row = plan.slots * ye
+        total = rec_ref[0, 0, 0, e_row:e_row + 1, :]
+        for t in range(1, plan.n_chip):
+            total = total + rec_ref[t, 0, 0, e_row:e_row + 1, :]
+        own_ref[0, 0, Z_BATCH - 1, 0:1, :] = total
+        send_ref[0, 0, Z_BATCH - 1, 0:1, :] = total
+
+
+def zi_call(plan, core, rec, wi):
+    shape = jax.ShapeDtypeStruct((3, 2, plan.y_even, plan.k_pad, LANES), F32)
+    spec = pl.BlockSpec((3, 2, Z_BATCH, plan.k_pad, LANES), lambda i: (0, 0, i, 0, 0))
+    return pl.pallas_call(
+        functools.partial(zi_kernel, plan), grid=(plan.y_even // Z_BATCH,), out_shape=(shape, shape),
+        in_specs=[SMEM_SPEC, pl.BlockSpec(rec.shape, lambda i: (0,) * 5), pl.BlockSpec(wi.shape, lambda i: (0,) * 4)],
+        out_specs=(spec, spec),
+        scratch_shapes=[pltpu.VMEM((2, Z_BATCH, plan.k_pad, 2 * plan.n), F32)],
+        compiler_params=pltpu.CompilerParams(vmem_limit_bytes=VMEM_BIG), name="idft_z",
+    )(core, rec, wi)
+
+
+def field_kernel(plan, n_blk, n_xt, e_norm, core_ref, table_ref, num_ref, slot_ref, own_ref, rec_ref, mi_ref,
+                 out_ref, energy_ref, fhm_ref, flo_ref, lhs_ref):
+    core = core_ref[0]
+    kp = plan.k_pad
+    for m in range(3):
+        for kind in range(2):
+            lhs_ref[m, kind] = jnp.concatenate([mi_ref[m, core, kind], mi_ref[m, 1 - core, kind]], axis=1)
+
+    def column(c, y):
+        return jnp.concatenate([own_ref[c, 0, y], own_ref[c, 1, y], rec_ref[c, 0, y], rec_ref[c, 1, y]], axis=0)
+
+    def put(res, spots):
+        hi, mid, lo = split3(res)
+        for pos, (y, c) in enumerate(spots):
+            ln = slice(pos * LANES, (pos + 1) * LANES)
+            fhm_ref[y, c, :, :LANES] = hi[:, ln]
+            fhm_ref[y, c, :, LANES:] = mid[:, ln]
+            flo_ref[y, c] = lo[:, ln]
+
+    def planes(step, carry):
+        y0 = 2 * step
+        data = jnp.concatenate([column(0, y0), column(0, y0 + 1)], axis=1)
+        put(mul6([lhs_ref[m, 0] for m in range(3)], split3(data)), ((y0, 0), (y0 + 1, 0)))
+        for y in (y0, y0 + 1):
+            data = jnp.concatenate([column(1, y), column(2, y)], axis=1)
+            put(mul6([lhs_ref[m, 1] for m in range(3)], split3(data)), ((y, 1), (y, 2)))
+        return carry
+    lax.fori_loop(0, plan.y_even // 2, planes, 0)
+    lanes = own_ref[0, 0, plan.y_even - 1, 0:1, :] + rec_ref[0, 0, plan.y_even - 1, 0:1, :]
+    energy_ref[...] = jnp.broadcast_to(jnp.sum(lanes, axis=1, keepdims=True) * e_norm, energy_ref.shape)
+    interp_kernel(n_blk, n_xt, table_ref, num_ref, slot_ref, fhm_ref, flo_ref, out_ref)
+
+
+def field_call(plan, core, table, num, slots, own, rec, mi, n_blk, n_xt, e_norm):
+    return pl.pallas_call(
+        functools.partial(field_kernel, plan, n_blk, n_xt, e_norm),
+        out_shape=(jax.ShapeDtypeStruct((3, 128, LANES), F32), jax.ShapeDtypeStruct((8, LANES), F32)),
+        in_specs=[SMEM_SPEC, SMEM_SPEC, SMEM_SPEC] + [VMEM_SPEC] * 4, out_specs=(VMEM_SPEC, VMEM_SPEC),
+        scratch_shapes=[pltpu.VMEM((plan.y_even, 3, plan.x_pad, 2 * LANES), BF16),
+                        pltpu.VMEM((plan.y_even, 3, plan.x_pad, LANES), BF16),
+                        pltpu.VMEM((3, 2, plan.x_pad, 4 * plan.k_pad), BF16)],
+        compiler_params=pltpu.CompilerParams(vmem_limit_bytes=VMEM_BIG), name="idft_x_interp",
+    )(core, table, num, slots, own, rec, mi)
 
 
 def solution(mesh):
-    n_rows = mesh.shape["row"]
     n_cols = mesh.shape["col"]
-    slot_axes = ("rep", "col", "row")
-    to_next_row = [(k, (k + 1) % n_rows) for k in range(n_rows)]
-    to_prev_row = [(k, (k - 1) % n_rows) for k in range(n_rows)]
-    to_next_col = [(k, (k + 1) % n_cols) for k in range(n_cols)]
-    to_prev_col = [(k, (k - 1) % n_cols) for k in range(n_cols)]
+    n_cx = mesh.shape["row"] // 2
+    fine = jax.sharding.Mesh(mesh.devices.reshape(mesh.shape["rep"], n_cols, n_cx, 2), ("rep", "col", "cx", "core"))
+    slot_axes = ("rep", "col", "cx", "core")
+    chip_axes = ("cx", "col")
+    turn = [(a * 2 + b, b * 2 + a) for a in range(n_cols) for b in range(2)]
+    other_core = [(0, 1), (1, 0)]
 
     def device_body(part_mass, cell_idx, cic_wts, live_mask, gas_block):
         grid_size, y_blk, z_blk = gas_block.shape
         per_dev = part_mass.shape[0]
-        n_slots = per_dev * n_rows * n_cols
-        row_id = lax.axis_index("row")
-        col_id = lax.axis_index("col")
+        n_chip = n_cx * n_cols
+        n_slots = per_dev * n_chip * 2
+        plan = Plan(grid_size, n_chip, y_blk, z_blk)
+        tab = plan.tables()
+        core = lax.axis_index("core").astype(jnp.int32)
+        chip = (lax.axis_index("cx") * n_cols + lax.axis_index("col")).astype(jnp.int32)
+        core_arr = core.reshape(1)
+        base = (core * plan.per_core + chip * plan.slots).reshape(1)
         n_xt = grid_size // X_TILE
         n_blk = y_blk * n_xt
-        raw = slot_arrays(part_mass, cell_idx, cic_wts, live_mask, y_blk)
+
+        raw = lax.ppermute(slot_arrays(part_mass, cell_idx, cic_wts, live_mask, y_blk), ("col", "core"), turn)
+        gas = lax.ppermute(jnp.transpose(gas_block, (1, 0, 2)), ("col", "core"), turn)
         table, num = pair_table(raw[0].reshape(-1), n_blk, n_xt)
         slots = sort_call(jnp.concatenate([raw, home_ranks()[None]]))
-        rho = deposit_call(table, num, slots, y_blk + 1, grid_size, n_blk, n_xt)
-        spread = jnp.transpose(rho[:, :grid_size, :z_blk + 1], (1, 0, 2))
-        from_row = lax.ppermute(spread[:, y_blk, :], "row", to_next_row)
-        body_y = jnp.concatenate([spread[:, 0:1, :] + from_row[:, None, :], spread[:, 1:y_blk, :]], axis=1)
-        from_col = lax.ppermute(body_y[:, :, z_blk], "col", to_next_col)
-        density = jnp.concatenate([body_y[:, :, 0:1] + from_col[:, :, None], body_y[:, :, 1:z_blk]], axis=2) + gas_block
-
-        full_ids = jnp.arange(grid_size)
-        fwd_mat = complex_matrix(full_ids, grid_size, -1.0)
-        stage_x = dft_apply("pkx,xyz->pkyz", fwd_mat[:, 0], density)
-        swap_a = lax.all_to_all(stage_x, "row", 1, 2, tiled=True)
-        stage_y = dft_apply("pqly,qkyz->plkz", fwd_mat, swap_a)
-        swap_b = lax.all_to_all(stage_y, "col", 1, 3, tiled=True)
-        rho_hat = dft_apply("pqmz,qlkz->pmlk", fwd_mat, swap_b)
-
-        k_unit = 2.0 * math.pi / grid_size
-        kz_n = wave_numbers(full_ids, grid_size)
-        ky_n = wave_numbers(col_id * (grid_size // n_cols) + jnp.arange(grid_size // n_cols), grid_size)
-        kx_n = wave_numbers(row_id * (grid_size // n_rows) + jnp.arange(grid_size // n_rows), grid_size)
-        norm_sq = kz_n[:, None, None] ** 2 + ky_n[None, :, None] ** 2 + kx_n[None, None, :] ** 2
-        influence = influence_of(norm_sq, grid_size)
-        local_sum = jnp.sum(influence * (rho_hat[0] * rho_hat[0] + rho_hat[1] * rho_hat[1]))
-        energy = lax.psum(local_sum, ("row", "col")) * (0.5 / (grid_size ** 3 * n_slots))
-        i_pot = jnp.stack([-influence * rho_hat[1], influence * rho_hat[0]])
-        deriv_hat = jnp.stack([i_pot * (k_unit * kx_n)[None, None, None, :],
-                               i_pot * (k_unit * ky_n)[None, None, :, None],
-                               i_pot * (k_unit * kz_n)[None, :, None, None]], axis=2)
-
-        inv_mat = complex_matrix(full_ids, grid_size, 1.0)
-        back_z = dft_apply("pqnm,qmclk->pnclk", inv_mat, deriv_hat)
-        swap_c = lax.all_to_all(back_z, "col", 1, 3, tiled=True)
-        back_y = dft_apply("pqyl,qzclk->pyzck", inv_mat, swap_c)
-        swap_d = lax.all_to_all(back_y, "row", 1, 4, tiled=True)
-        cos_t, sin_t = dft_table(full_ids, grid_size, 1.0)
-        real_mat = jnp.stack([cos_t, -sin_t]) * (1.0 / grid_size ** 3)
-        fields = dft_apply("qxk,qyzck->ycxz", real_mat, swap_d)
-
-        from_row_next = lax.ppermute(fields[0:1], "row", to_prev_row)
-        ext_y = jnp.concatenate([fields, from_row_next], axis=0)
-        from_col_next = lax.ppermute(ext_y[..., 0:1], "col", to_prev_col)
-        ext = jnp.concatenate([ext_y, from_col_next, jnp.zeros(ext_y.shape[:3] + (LANES - z_blk - 1,), F32)], axis=3)
-        ext = jnp.concatenate([ext, ext[:, :, :16]], axis=2)
-        hi = lax.reduce_precision(ext, 8, 7)
-        mid = lax.reduce_precision(ext - hi, 8, 7)
-        low = ext - hi - mid
-        fhm = jnp.concatenate([hi, mid], axis=3).astype(BF16)
-        forces = interp_call(table, num, slots, fhm, low.astype(BF16), n_blk, n_xt)
+        rho = deposit_call(table, num, slots, plan.y_even, grid_size, n_blk, n_xt)
+        own, send = x_call(plan, core_arr, rho, gas, tab["mx"])
+        rec = lax.ppermute(send, "core", other_core)
+        to_y = z_call(plan, core_arr, own, rec, tab["wz"])
+        at_y = lax.all_to_all(to_y, chip_axes, 0, 0, tiled=True)
+        from_y = y_call(plan, base, at_y, tab["my"], tab["ei"])
+        at_z = lax.all_to_all(from_y, chip_axes, 0, 0, tiled=True)
+        own, send = zi_call(plan, core_arr, at_z, tab["wi"])
+        rec = lax.ppermute(send, "core", other_core)
+        e_norm = 0.5 / (grid_size ** 3 * n_slots)
+        forces, energy = field_call(plan, core_arr, table, num, slots, own, rec, tab["mi"], n_blk, n_xt, e_norm)
         back = sort_call(jnp.concatenate([slots[5:6], forces]))
-        part_force = back[1:4].reshape(3, per_dev).T
-        return part_force, energy.reshape(1)
+        home = lax.ppermute(back[1:4], ("col", "core"), turn)
+        return home.reshape(3, per_dev).T, energy[0, 0:1]
 
     return jax.shard_map(
-        device_body, mesh=mesh,
-        in_specs=(P(slot_axes), P(slot_axes, None), P(slot_axes, None, None), P(slot_axes), P("rep", "row", "col")),
+        device_body, mesh=fine,
+        in_specs=(P(slot_axes), P(slot_axes, None), P(slot_axes, None, None), P(slot_axes), P("rep", ("cx", "core"), "col")),
         out_specs=(P(slot_axes, None), P("rep")), check_vma=False)

time: 1580 us -> 517 us (0.33)
  waiting for transfers between devices: 416 us -> 63 us
  blocking collectives: 444 us -> 94.3 us
  local copies, waits for them, and re-layouts: 258 us -> 11.9 us
  matrix products: 181 us -> 0 us
  Pallas kernels: 150 us -> 273 us
  other arithmetic: 93.1 us -> 5.43 us
  starting transfers between devices: 20.3 us -> 65.1 us
    all_to_all x2 -> x1, waiting for transfers between devices: 407 us -> 44.7 us  [device_body(): at_y = lax.all_to_all(to_y, chip_axes, 0, 0, tiled=True)]
    all_to_all x2 -> x1, blocking collectives: 420 us -> 94.3 us  [device_body(): at_z = lax.all_to_all(from_y, chip_axes, 0, 0, tiled=True)]
    dot_general x6 -> x0, matrix products: 181 us -> none  [dft_apply(): jnp.einsum(form, lhs_mat, rhs_arr, precision=MATMUL_PREC, preferred_eleme...]
    all_to_all x6 -> x0, local copies, waits for them, and re-layouts: 137 us -> none  [the longest x2 80.6 us: device_body(): swap_c = lax.all_to_all(back_z, 'col', 1, 3, tiled=True)]
    pallas_call x1 -> x5, Pallas kernels: 71.8 us -> 196 us  [the longest x1 87.4 us: field_call(): pl.pallas_call(functools.partial(field_kernel, plan, n_blk, n_xt, e_norm)...]
    dot_general x5 -> x0, local copies, waits for them, and re-layouts: 83.4 us -> none  [dft_apply(): jnp.einsum(form, lhs_mat, rhs_arr, precision=MATMUL_PREC, preferred_eleme...]
    ppermute x4 -> x5, starting transfers between devices: 0.39 us -> 47.6 us  [the longest x1 36.9 us: device_body(): lax.ppermute(jnp.transpose(gas_block, (1, 0, 2)), ('col', 'core'), turn)]
    convert_element_type x1, other arithmetic: 29.5 us -> 0.08 us  [home_ranks(): return (a * 128 + (b & 7) * 16 + (b >> 3)).astype(F32)]
  transfers between devices with their start and end apart: 6 -> 6, of which waited for: 5 -> 3; matrix products, arithmetic and copies ran while one was open for 1% -> 1% of each run, Pallas kernels for 0% -> 13%
where the time goes in v2:
time: 517 us; the launch traced here: 513 us
  Pallas kernels  273 us (53%)
  blocking collectives  94.3 us (18%)
  starting transfers between devices  65.1 us (13%)
  waiting for transfers between devices  63 us (12%)
  local copies, waits for them, and re-layouts  11.9 us (2%)
  other arithmetic  5.43 us (1%)
    all_to_all x1, blocking collectives, device_body(): at_z = lax.all_to_all(from_y, chip_axes, 0, 0, tiled=True)  94.3 us
    pallas_call x1, Pallas kernels, field_call(): pl.pallas_call(functools.partial(field_kernel, plan, n_blk, n_xt, e_norm)...  87.4 us
    pallas_call x1, Pallas kernels, deposit_call(): pl.pallas_call(functools.partial(deposit_kernel, n_blk, n_xt, grid_size),...  55.3 us
    all_to_all x1, waiting for transfers between devices, device_body(): at_y = lax.all_to_all(to_y, chip_axes, 0, 0, tiled=True)  44.7 us
    pallas_call x1, Pallas kernels, y_call(): pl.pallas_call(functools.partial(y_kernel, plan), out_shape=jax.ShapeDtyp...  38.2 us
    ppermute x1, starting transfers between devices, device_body(): lax.ppermute(jnp.transpose(gas_block, (1, 0, 2)), ('col', 'core'), turn)  36.9 us
    pallas_call x1, Pallas kernels, zi_call(): pl.pallas_call(functools.partial(zi_kernel, plan), grid=(plan.y_even // Z...  34.3 us
    pallas_call x2, Pallas kernels, sort_call(): pl.pallas_call(functools.partial(sort_kernel, n_arr), out_shape=jax.Shape...  21.8 us
  transfers between devices with their start and end apart: 6, of which 3 were waited for; matrix products, arithmetic and copies ran while one was open for 1% of the time, Pallas kernels for 13%

profile of v2, /device:TPU:0, one launch (start us, length us, event | category | flops | bytes accessed | tf_op | source)
XLA Modules:
  0.0 513.1 jit_solution(16414306129886873669)
XLA Ops:
  0.6 0.0 copy-start.3
  0.6 0.0 copy-start.2
  0.7 0.0 copy-start.1
  0.7 0.0 copy-start.4
  0.7 6.1 %copy.21 = f32[192,48,96]{2,0,1:T(8,128)} copy(f32[192,48,96]{2,1,0:T(8,128)} %param.15) | data formatting | bytes 7077888 | tf_op args[4]
  6.8 36.9 %collective-permute-start.1 = (f32[48,192,96]{2,1,0:T(8,128)}, f32[48,192,96]{2,1,0:T(8,128)}, u32[]{:S(2)}, u32[]{:S(2)}) collective-permute-start(f32[48,192,96]{2,1,0:T(8,128)} %bitcast.25), channel_id=1, source_target_pairs={{0,0},{1,4},{4,1},{5,5},{2,2},{3,6},{6,3},{7,7}} | collective-permute-start | bytes 10616840 | tf_op jit(solution)/shard_map/ppermute | solution.py:607
  43.8 0.0 copy-done.3
  43.8 0.2 slice.46
  44.0 0.1 copy.23
  44.1 0.1 fusion.6
  44.3 0.0 copy-done.2
  44.3 0.1 slice_or_fusion
  44.5 0.7 collective-permute-start
  45.2 0.1 add_convert_fusion
  45.3 0.0 collective-permute-done
  45.4 1.1 convert_reduce_fusion
  46.4 0.1 compare_select_fusion.2
  46.5 0.1 select_reduce_fusion.1
  46.6 0.7 slice.54.num_ref
  47.3 0.8 pad_maximum_fusion.in_ref
  48.1 12.3 %slot_sort.2.slot_ref = f32[6,128,128]{2,1,0:T(8,128)} custom-call(f32[6,128,128]{2,1,0:T(8,128)} %pad_maximum_fusion.in_ref), custom_call_target="tpu_custom_call" | custom-call | tf_op jit(solution)/shard_map/slot_sort/pallas_call | solution.py:96
  60.3 0.1 convert_reduce_fusion.1
  60.5 0.1 select_reduce_fusion
  60.6 0.7 compare_select_fusion
  61.3 0.6 pad_add_fusion.table_ref
  61.8 55.3 %deposit.1.rho_ref = f32[50,208,128]{2,1,0:T(8,128)} custom-call(s32[2,224]{1,0:T(2,128)} %pad_add_fusion.table_ref, s32[1]{0:T(128)} %slice.54.num_ref, f32[6,128,128]{2,1,0:T(8,128)} %slot_sort.2.slot_ref), custom_call_target="tpu_custom_call" | custom-call | tf_op jit(solution)/shard_map/deposit/pallas_call | solution.py:213
  117.1 0.0 collective-permute-done.1.gas_ref
  117.1 20.8 %dft_x.1 = (f32[2,50,56,128]{3,2,1,0:T(8,128)}, f32[2,50,56,128]{3,2,1,0:T(8,128)}) custom-call(s32[1]{0:T(128)} %bitcast.6.core_ref, f32[50,208,128]{2,1,0:T(8,128)} %deposit.1.rho_ref, f32[48,192,96]{2,1,0:T(8,128)} %collective-permute-done.1.gas_ref, bf16[3,2,112,192]{3,2,1,0:T(8,128)(2,1)} %constant.99.clone.mx_ref), custom_call_target="tpu_custom_call" | custom-call | tf_op jit(solution)/shard_map/dft_x/pallas_call | solution.py:364
  137.9 9.3 %collective-permute-start.2 = (f32[2,50,56,128]{3,2,1,0:T(8,128)}, f32[2,50,56,128]{3,2,1,0:T(8,128)S(1)}, u32[]{:S(2)}, u32[]{:S(2)}) collective-permute-start(f32[2,50,56,128]{3,2,1,0:T(8,128)} %get-tuple-element.9), channel_id=1, source_target_pairs={{0,1},{1,0},{2,3},{3,2},{4,5},{5,4},{6,7},{7,6}} | collective-permute-start | bytes 8601608 | tf_op jit(solution)/shard_map/ppermute | solution.py:612
  147.2 4.9 collective-permute-done.2.rec_ref
  152.1 1.6 copy-done
  153.7 14.9 %dft_z.1 = f32[4,3,640,128]{3,2,1,0:T(8,128)} custom-call(s32[1]{0:T(128)} %bitcast.6.core_ref, f32[2,50,56,128]{3,2,1,0:T(8,128)} %get-tuple-element.8.own_ref, f32[2,50,56,128]{3,2,1,0:T(8,128)} %copy-done, bf16[3,2,2,128,384]{4,3,2,1,0:T(8,128)(2,1)} %constant.100.clone.wz_ref), custom_call_target="tpu_custom_call" | custom-call | tf_op jit(solution)/shard_map/dft_z/pallas_call | solution.py:408
  168.6 17.5 %all-to-all-start = ((f32[4,3,640,128]{3,2,1,0:T(8,128)}), f32[4,3,640,128]{3,2,1,0:T(8,128)}, u32[]{:S(2)}, u32[]{:S(2)}) async-start(f32[4,3,640,128]{3,2,1,0:T(8,128)} %dft_z.1), calls=%async_computation | async-start | bytes 7864320 | tf_op jit(solution)/shard_map/all_to_all | solution.py:614
  186.1 44.7 %all-to-all-done.rec_ref = f32[4,3,640,128]{3,2,1,0:T(8,128)} async-done(((f32[4,3,640,128]{3,2,1,0:T(8,128)}), f32[4,3,640,128]{3,2,1,0:T(8,128)}, u32[]{:S(2)}, u32[]{:S(2)}) %all-to-all-start) | async-done | bytes 3932192 | tf_op jit(solution)/shard_map/all_to_all | solution.py:614
  230.8 38.2 %dft_y.1 = f32[4,2,3,640,128]{4,3,2,1,0:T(8,128)} custom-call(s32[1]{0:T(128)} %bitcast.11.base_ref, f32[4,3,640,128]{3,2,1,0:T(8,128)} %all-to-all-done.rec_ref, bf16[3,384,224]{2,1,0:T(8,128)(2,1)} %constant.101.clone.my_ref, bf16[3,4,224,192]{3,2,1,0:T(8,128)(2,1)} %constant.102.clone.ei_ref), custom_call_target="tpu_custom_call" | custom-call | tf_op jit(solution)/shard_map/dft_y/pallas_call | solution.py:479
  269.0 94.3 %all_to_all.10.rec_ref = f32[4,2,3,640,128]{4,3,2,1,0:T(8,128)} all-to-all(f32[4,2,3,640,128]{4,3,2,1,0:T(8,128)} %dft_y.1), channel_id=1, replica_groups=mesh['rep'=1,'col'=2,'cx'=2,'core'=2] {'cx','col'}, dimensions={0} | all-to-all | bytes 15728640 | tf_op jit(solution)/shard_map/all_to_all | solution.py:616
  363.2 34.3 %idft_z.1 = (f32[3,2,50,56,128]{4,3,2,1,0:T(8,128)}, f32[3,2,50,56,128]{4,3,2,1,0:T(8,128)}) custom-call(s32[1]{0:T(128)} %bitcast.6.core_ref, f32[4,2,3,640,128]{4,3,2,1,0:T(8,128)} %all_to_all.10.rec_ref, bf16[3,2,384,512]{3,2,1,0:T(8,128)(2,1)} %constant.103.clone.wi_ref), custom_call_target="tpu_custom_call" | custom-call | tf_op jit(solution)/shard_map/idft_z/pallas_call | solution.py:529
  397.6 0.0 collective-permute-start.3
  397.6 13.4 %collective-permute-done.3.rec_ref = f32[3,2,50,56,128]{4,3,2,1,0:T(8,128)} collective-permute-done((f32[3,2,50,56,128]{4,3,2,1,0:T(8,128)}, f32[3,2,50,56,128]{4,3,2,1,0:T(8,128)}, u32[]{:S(2)}, u32[]{:S(2)}) %collective-permute-start.3) | collective-permute-done | bytes 8601632 | tf_op jit(solution)/shard_map/ppermute | solution.py:618
  411.0 87.4 %idft_x_interp.1 = (f32[3,128,128]{2,1,0:T(8,128)}, f32[8,128]{1,0:T(8,128)}) custom-call(s32[1]{0:T(128)} %bitcast.6.core_ref, s32[2,224]{1,0:T(2,128)} %pad_add_fusion.table_ref, s32[1]{0:T(128)} %slice.54.num_ref, f32[6,128,128]{2,1,0:T(8,128)} %slot_sort.2.slot_ref, f32[3,2,50,56,128]{4,3,2,1,0:T(8,128)} %get-tuple-element.10.own_ref, ...), custom_call_target="tpu_custom_call" | custom-call | tf_op jit(solution)/shard_map/idft_x_interp/pallas_call | solution.py:572
  498.3 0.0 slice-done
  498.4 1.6 pad_maximum_fusion.1.in_ref
  500.0 9.5 %slot_sort.3 = f32[4,128,128]{2,1,0:T(8,128)} custom-call(f32[4,128,128]{2,1,0:T(8,128)} %pad_maximum_fusion.1.in_ref), custom_call_target="tpu_custom_call" | custom-call | tf_op jit(solution)/shard_map/slot_sort/pallas_call | solution.py:96
  509.5 0.9 slice.62
  510.4 0.7 collective-permute-start.4
  511.1 1.2 slice.56
  512.3 0.0 collective-permute-done.4
  512.3 0.8 copy.22
  (14 shorter events, 0.1 us)
Async XLA Ops:
  0.6 43.1 %copy-start.3 = (f32[16384,3,2]{0,2,1:T(2,128)S(1)}, f32[16384,3,2]{0,2,1:T(2,128)}, u32[]{:S(2)}) copy-start(f32[16384,3,2]{0,2,1:T(2,128)} %param.13) | copy-start | bytes 1179652
  0.6 43.6 %copy-start.2 = (s32[16384,3]{0,1:T(4,128)S(1)}, s32[16384,3]{0,1:T(4,128)}, u32[]{:S(2)}) copy-start(s32[16384,3]{0,1:T(4,128)} %param.12) | copy-start | bytes 589828
  0.7 43.8 %copy-start.1 = (s32[16384]{0:T(1024)S(1)}, s32[16384]{0:T(1024)}, u32[]{:S(2)}) copy-start(s32[16384]{0:T(1024)} %param.14) | copy-start | bytes 196612
  0.7 43.8 %copy-start.4 = (f32[16384]{0:T(1024)S(1)}, f32[16384]{0:T(1024)}, u32[]{:S(2)}) copy-start(f32[16384]{0:T(1024)} %param.11) | copy-start | bytes 196612
  6.8 110.3 %collective-permute-start.1 = (f32[48,192,96]{2,1,0:T(8,128)}, f32[48,192,96]{2,1,0:T(8,128)}, u32[]{:S(2)}, u32[]{:S(2)}) collective-permute-start(f32[48,192,96]{2,1,0:T(8,128)} %bitcast.25), channel_id=1, source_target_pairs={{0,0},{1,4},{4,1},{5,5},{2,2},{3,6},{6,3},{7,7}} | collective-permute-start | bytes 10616840 | tf_op jit(solution)/shard_map/ppermute | solution.py:607
  44.5 0.8 collective-permute-start
  137.9 14.2 %collective-permute-start.2 = (f32[2,50,56,128]{3,2,1,0:T(8,128)}, f32[2,50,56,128]{3,2,1,0:T(8,128)S(1)}, u32[]{:S(2)}, u32[]{:S(2)}) collective-permute-start(f32[2,50,56,128]{3,2,1,0:T(8,128)} %get-tuple-element.9), channel_id=1, source_target_pairs={{0,1},{1,0},{2,3},{3,2},{4,5},{5,4},{6,7},{7,6}} | collective-permute-start | bytes 8601608 | tf_op jit(solution)/shard_map/ppermute | solution.py:612
  152.1 1.6 copy-start
  168.6 62.1 %all-to-all-start = ((f32[4,3,640,128]{3,2,1,0:T(8,128)}), f32[4,3,640,128]{3,2,1,0:T(8,128)}, u32[]{:S(2)}, u32[]{:S(2)}) async-start(f32[4,3,640,128]{3,2,1,0:T(8,128)} %dft_z.1), calls=%async_computation | async-start | bytes 7864320 | tf_op jit(solution)/shard_map/all_to_all | solution.py:614
  397.6 13.4 %collective-permute-start.3 = (f32[3,2,50,56,128]{4,3,2,1,0:T(8,128)}, f32[3,2,50,56,128]{4,3,2,1,0:T(8,128)}, u32[]{:S(2)}, u32[]{:S(2)}) collective-permute-start(f32[3,2,50,56,128]{4,3,2,1,0:T(8,128)} %get-tuple-element.11), channel_id=1, source_target_pairs={{0,1},{1,0},{2,3},{3,2},{4,5},{5,4},{6,7},{7,6}} | collective-permute-start | bytes 25804808 | tf_op jit(solution)/shard_map/ppermute | solution.py:618
  411.0 87.4 %slice-start = ((f32[6,128,128]{2,1,0:T(8,128)}), f32[1,128,128]{2,1,0:T(8,128)S(1)}, s32[]{:S(2)}) async-start(f32[6,128,128]{2,1,0:T(8,128)} %slot_sort.2.slot_ref), calls=%async_computation.2 | async-start | bytes 131072 | tf_op jit(solution)/shard_map/slice | solution.py:621
  510.4 1.9 collective-permute-start.4

commit v3 on v2

--- a/solution.py
+++ b/solution.py
@@ -31,17 +31,18 @@
 def bitonic(bufs):
     sub = lax.broadcasted_iota(jnp.int32, (8, LANES), 0)
     lane = lax.broadcasted_iota(jnp.int32, (8, LANES), 1)
-    base = lane * 128 + sub * 16
+    base = lane * 128 + sub
 
     def bit(rank, pos):
         return lax.shift_right_logical(rank, jnp.full_like(rank, pos)) & 1
 
     def vreg_stage(k, j):
+        step = 1 << (j - 3)
         for v in range(16):
-            if v & (1 << j):
+            if v & step:
                 continue
-            low, high = pl.ds(8 * v, 8), pl.ds(8 * (v + (1 << j)), 8)
-            sgn = 1.0 - 2.0 * bit(base + v, k).astype(F32)
+            low, high = pl.ds(8 * v, 8), pl.ds(8 * (v + step), 8)
+            sgn = 1.0 - 2.0 * bit(base + 8 * v, k).astype(F32)
             a = [b[low, :] for b in bufs]
             c = [b[high, :] for b in bufs]
             swap = a[0] * sgn > c[0] * sgn
@@ -55,19 +56,22 @@
         keep_low = upper == 0
         for v in range(16):
             rows = pl.ds(8 * v, 8)
-            sgn = 1.0 - 2.0 * (bit(base + v, k) ^ upper).astype(F32)
+            sgn = 1.0 - 2.0 * (bit(base + 8 * v, k) ^ upper).astype(F32)
             own = [b[rows, :] for b in bufs]
             other = [jnp.where(keep_low, pltpu.roll(o, size - dist, axis), pltpu.roll(o, dist, axis)) for o in own]
             take = other[0] * sgn < own[0] * sgn
             for b, o, p in zip(bufs, own, other):
                 b[rows, :] = jnp.where(take, p, o)
 
+    def stage(k, j):
+        if j >= 3:
+            vreg_stage(k, j)
+        else:
+            roll_stage(k, j, 1 << j, 0)
+
     for k in range(1, 8):
         for j in range(k - 1, -1, -1):
-            if j >= 4:
-                roll_stage(k, j, 1 << (j - 4), 0)
-            else:
-                vreg_stage(k, j)
+            stage(k, j)
 
     def phase(k, carry):
         def lane_stage(step, c):
@@ -75,32 +79,36 @@
             roll_stage(k, j, jnp.left_shift(1, j - 7), 1)
             return c
         lax.fori_loop(0, k - 7, lane_stage, 0)
-        for j in (6, 5, 4):
-            roll_stage(k, j, 1 << (j - 4), 0)
-        for j in (3, 2, 1, 0):
-            vreg_stage(k, j)
+        for j in range(6, -1, -1):
+            stage(k, j)
         return carry
     lax.fori_loop(8, 15, phase, 0)
 
 
-def sort_kernel(n_arr, in_ref, out_ref, *bufs):
-    for n in range(n_arr):
+CHUNKS = 128
+SLOT_ROWS = 8 * (CHUNKS + 1)
+
+
+def sort_kernel(in_ref, out_ref, *bufs):
+    for n in range(5):
         bufs[n][...] = in_ref[n]
+    row = lax.broadcasted_iota(jnp.int32, (CHUNKS, LANES), 0)
+    col = lax.broadcasted_iota(jnp.int32, (CHUNKS, LANES), 1)
+    bufs[5][...] = (row * LANES + col).astype(F32)
     bitonic(bufs)
-    for n in range(n_arr):
-        out_ref[n] = bufs[n][...].T
-
-
-def sort_call(stacked):
-    n_arr = stacked.shape[0]
-    return pl.pallas_call(
-        functools.partial(sort_kernel, n_arr),
-        out_shape=jax.ShapeDtypeStruct(stacked.shape, F32),
-        in_specs=[pl.BlockSpec(memory_space=pltpu.VMEM)],
-        out_specs=pl.BlockSpec(memory_space=pltpu.VMEM),
-        scratch_shapes=[pltpu.VMEM((128, LANES), F32)] * n_arr,
-        name="slot_sort",
-    )(stacked)
+    zero = jnp.zeros((CHUNKS, LANES), F32)
+    for n in range(8):
+        out_ref[pl.ds(n, CHUNKS, stride=8), :] = bufs[n][...].T if n < 6 else zero
+    out_ref[8 * CHUNKS:, :] = jnp.zeros((8, LANES), F32)
+
+
+def unsort_kernel(slot_ref, force_ref, out_ref, *bufs):
+    bufs[0][...] = slot_ref[pl.ds(5, CHUNKS, stride=8), :]
+    for n in range(3):
+        bufs[n + 1][...] = force_ref[pl.ds(n, CHUNKS, stride=8), :]
+    bitonic(bufs)
+    for n in range(3):
+        out_ref[n] = bufs[n + 1][...].T
 
 
 def pair_table(key, n_blk, n_xt):
@@ -108,36 +116,42 @@
     bounds = ((b_ids // n_xt) << Y_SHIFT) | (((b_ids % n_xt) * X_TILE) << X_SHIFT)
     starts = jnp.sum((key[None, :] < bounds[:, None].astype(F32)).astype(jnp.int32), axis=1)
     first, last = starts[:-1], starts[1:]
-    lo = first // LANES
-    count = jnp.where(last > first, (last + LANES - 1) // LANES - lo, 0)
+    count = (last - first + LANES - 1) // LANES
     ids = jnp.arange(n_blk)
     ends = jnp.sum(jnp.where(ids[None, :] <= ids[:, None], count[None, :], 0), axis=1)
-    t_max = n_blk + 128
-    t_ids = jnp.arange(t_max)
+    t_ids = jnp.arange(n_blk + CHUNKS)
     blk = jnp.sum((ends[None, :] <= t_ids[:, None]).astype(jnp.int32), axis=1)
-    chunk = t_ids + jnp.sum(jnp.where(ids[None, :] == blk[:, None], (lo - ends + count)[None, :], 0), axis=1)
+    hot = ids[None, :] == blk[:, None]
+    beg = jnp.sum(jnp.where(hot, (first - LANES * (ends - count))[None, :], 0), axis=1) + LANES * t_ids
+    size = jnp.minimum(jnp.sum(jnp.where(hot, last[None, :], 0), axis=1) - beg, LANES)
     live = t_ids < ends[-1]
-    table = jnp.stack([jnp.where(live, blk, n_blk + 7), jnp.where(live, chunk, 0)])
+    table = jnp.stack([jnp.where(live, blk, 0), jnp.where(live, beg, 0), jnp.where(live, size, 0)])
     return table.astype(jnp.int32), ends[-1:].astype(jnp.int32)
 
 
-def read_pair(t, table_ref, slot_ref, n_blk, n_xt):
+def read_window(t, table_ref, slot_ref, n_xt):
     blk = table_ref[0, t]
-    chunk = table_ref[1, t]
-    blk_in = jnp.minimum(blk, n_blk - 1)
-    y_pl = blk_in // n_xt
-    x_beg = pl.multiple_of((blk_in % n_xt) * X_TILE, 16)
-    code = slot_ref[0, pl.ds(chunk, 1), :].astype(jnp.int32)
+    beg = table_ref[1, t]
+    size = table_ref[2, t]
+    y_pl = blk // n_xt
+    x_beg = pl.multiple_of((blk % n_xt) * X_TILE, 16)
+    row = pl.multiple_of((beg >> 7) * 8, 8)
+    off = beg & 127
+    back = (LANES - off) & 127
+    lane = lax.broadcasted_iota(jnp.int32, (8, LANES), 1)
+    win = jnp.where(lane < LANES - off, pltpu.roll(slot_ref[pl.ds(row, 8), :], back, 1),
+                    pltpu.roll(slot_ref[pl.ds(row + 8, 8), :], back, 1))
+    code = win[0:1].astype(jnp.int32)
     x_c = (code >> X_SHIFT) & 255
-    b_c = (code >> Y_SHIFT) * n_xt
-    for m in range(1, n_xt):
-        b_c = b_c + (x_c >= m * X_TILE).astype(jnp.int32)
-    mask = b_c == blk
-    vals = [slot_ref[n, pl.ds(chunk, 1), :] for n in range(1, 5)]
-    return chunk, y_pl, x_beg, x_c - x_beg, code & 127, mask, vals
-
-
-def deposit_kernel(n_blk, n_xt, grid_size, table_ref, num_ref, slot_ref, rho_ref):
+    vals = [win[n:n + 1] for n in range(1, 5)]
+    return row, off, size, lane, y_pl, x_beg, x_c - x_beg, code & 127, vals
+
+
+def spread_rows(row):
+    return jnp.broadcast_to(row, (16, LANES)).astype(BF16)
+
+
+def deposit_kernel(n_xt, grid_size, table_ref, num_ref, slot_ref, rho_ref):
     n_planes = rho_ref.shape[0]
 
     def clear(y, c):
@@ -148,16 +162,25 @@
     row_z = lax.broadcasted_iota(jnp.int32, (LANES, LANES), 0)
 
     def one(t):
-        chunk, y_pl, x_beg, x_l, z_c, mask, (q, wx, wy, wz) = read_pair(t, table_ref, slot_ref, n_blk, n_xt)
-        q = jnp.where(mask, q, 0.0)
+        row, off, size, lane, y_pl, x_beg, x_l, z_c, (q, wx, wy, wz) = read_window(t, table_ref, slot_ref, n_xt)
+        q = jnp.where(lane[0:1] < size, q, 0.0)
         pick_x = jnp.concatenate([(row_x == x_l).astype(F32), (row_x == x_l + 1).astype(F32)], axis=1).astype(BF16)
-        on_z = jnp.where(row_z == z_c, 1.0 - wz, jnp.where(row_z == z_c + 1, wz, 0.0))
-        rows = []
+        pick_z = [(row_z == z_c + c).astype(F32).astype(BF16).reshape(8, 16, LANES) for c in range(2)]
+        cols = [[], [], []]
         for w_y in (1.0 - wy, wy):
-            rows.append(jnp.concatenate([on_z * (q * (1.0 - wx) * w_y), on_z * (q * wx * w_y)], axis=1))
-        parts = split3(jnp.concatenate(rows, axis=0))
+            pieces = [[], [], []]
+            for w_x in (1.0 - wx, wx):
+                base = q * w_x * w_y
+                lower, upper = split3(base * (1.0 - wz)), split3(base * wz)
+                for m in range(3):
+                    low = spread_rows(lower[m].astype(F32))[None]
+                    high = spread_rows(upper[m].astype(F32))[None]
+                    pieces[m].append((pick_z[0] * low + pick_z[1] * high).reshape(LANES, LANES))
+            for m in range(3):
+                cols[m].append(jnp.concatenate(pieces[m], axis=1))
         res = None
-        for part in parts:
+        for m in (2, 1, 0):
+            part = jnp.concatenate(cols[m], axis=0)
             term = lax.dot_general(pick_x, part, (((1,), (1,)), ((), ())), preferred_element_type=F32)
             res = term if res is None else res + term
         for b in range(2):
@@ -175,28 +198,30 @@
     lax.fori_loop(0, n_planes, wrap, 0)
 
 
-def interp_kernel(n_blk, n_xt, table_ref, num_ref, slot_ref, fhm_ref, flo_ref, out_ref):
-    out_ref[...] = jnp.zeros(out_ref.shape, F32)
+def interp_kernel(n_xt, table_ref, num_ref, slot_ref, fhm_ref, flo_ref, out_ref):
     row_x = lax.broadcasted_iota(jnp.int32, (X_ROWS, LANES), 0)
     row_z = lax.broadcasted_iota(jnp.int32, (LANES, LANES), 0)
+    out_ref[...] = jnp.zeros(out_ref.shape, F32)
 
     def one(t):
-        chunk, y_pl, x_beg, x_l, z_c, mask, (q, wx, wy, wz) = read_pair(t, table_ref, slot_ref, n_blk, n_xt)
+        row, off, size, lane, y_pl, x_beg, x_l, z_c, (q, wx, wy, wz) = read_window(t, table_ref, slot_ref, n_xt)
         pick_z = jnp.concatenate([(row_z == z_c).astype(F32), (row_z == z_c + 1).astype(F32)], axis=1).astype(BF16)
         pick_2 = jnp.concatenate([pick_z, pick_z], axis=0)
         on_x = jnp.where(row_x == x_l, 1.0 - wx, jnp.where(row_x == x_l + 1, wx, 0.0))
         rows = pl.ds(x_beg, X_ROWS)
         wt = [on_x * (1.0 - wy), on_x * wy]
+        grads = []
         for comp in range(3):
-            acc = None
-            for b in range(2):
-                got = jnp.dot(fhm_ref[y_pl + b, comp, rows, :], pick_2, preferred_element_type=F32)
-                got = got + jnp.dot(flo_ref[y_pl + b, comp, rows, :], pick_z, preferred_element_type=F32)
-                term = (got[:, :LANES] * (1.0 - wz) + got[:, LANES:] * wz) * wt[b]
-                acc = term if acc is None else acc + term
-            grad = jnp.sum(acc, axis=0, keepdims=True)
-            here = pl.ds(chunk, 1)
-            out_ref[comp, here, :] = jnp.where(mask, -q * grad, out_ref[comp, here, :])
+            top = jnp.concatenate([fhm_ref[y_pl + b, comp, rows, :] for b in range(2)], axis=0)
+            low = jnp.concatenate([flo_ref[y_pl + b, comp, rows, :] for b in range(2)], axis=0)
+            got = jnp.dot(low, pick_z, preferred_element_type=F32) + jnp.dot(top, pick_2, preferred_element_type=F32)
+            got = got[:, :LANES] * (1.0 - wz) + got[:, LANES:] * wz
+            acc = got[:X_ROWS] * wt[0] + got[X_ROWS:] * wt[1]
+            grads.append(-q * jnp.sum(acc, axis=0, keepdims=True))
+        full = pltpu.roll(jnp.concatenate(grads + [jnp.zeros((5, LANES), F32)], axis=0), off, 1)
+        here, after = pl.ds(row, 8), pl.ds(row + 8, 8)
+        out_ref[here, :] = jnp.where((lane >= off) & (lane - off < size), full, out_ref[here, :])
+        out_ref[after, :] = jnp.where((lane < off) & (lane + LANES - off < size), full, out_ref[after, :])
 
     def body(t, c):
         one(2 * t)
@@ -209,22 +234,28 @@
 VMEM_SPEC = pl.BlockSpec(memory_space=pltpu.VMEM)
 
 
-def deposit_call(table, num, slots, y_ext, grid_size, n_blk, n_xt):
-    return pl.pallas_call(
-        functools.partial(deposit_kernel, n_blk, n_xt, grid_size),
+def sort_call(raw):
+    return pl.pallas_call(
+        sort_kernel, out_shape=jax.ShapeDtypeStruct((SLOT_ROWS, LANES), F32), in_specs=[VMEM_SPEC], out_specs=VMEM_SPEC,
+        scratch_shapes=[pltpu.VMEM((CHUNKS, LANES), F32)] * 6, name="slot_sort",
+    )(raw)
+
+
+def unsort_call(slots, forces):
+    return pl.pallas_call(
+        unsort_kernel, out_shape=jax.ShapeDtypeStruct((3, CHUNKS, LANES), F32),
+        in_specs=[VMEM_SPEC, VMEM_SPEC], out_specs=VMEM_SPEC,
+        scratch_shapes=[pltpu.VMEM((CHUNKS, LANES), F32)] * 4, name="slot_unsort",
+    )(slots, forces)
+
+
+def deposit_call(table, num, slots, y_ext, grid_size, n_xt):
+    return pl.pallas_call(
+        functools.partial(deposit_kernel, n_xt, grid_size),
         out_shape=jax.ShapeDtypeStruct((y_ext, grid_size + 16, LANES), F32),
         in_specs=[SMEM_SPEC, SMEM_SPEC, VMEM_SPEC], out_specs=VMEM_SPEC,
         compiler_params=pltpu.CompilerParams(vmem_limit_bytes=VMEM_BIG), name="deposit",
     )(table, num, slots)
-
-
-def interp_call(table, num, slots, fhm, flo, n_blk, n_xt):
-    return pl.pallas_call(
-        functools.partial(interp_kernel, n_blk, n_xt),
-        out_shape=jax.ShapeDtypeStruct((3, 128, LANES), F32),
-        in_specs=[SMEM_SPEC, SMEM_SPEC, VMEM_SPEC, VMEM_SPEC, VMEM_SPEC], out_specs=VMEM_SPEC,
-        compiler_params=pltpu.CompilerParams(vmem_limit_bytes=VMEM_BIG), name="interp",
-    )(table, num, slots, fhm, flo)
 
 
 def slot_arrays(part_mass, cell_idx, cic_wts, live_mask, y_blk):
@@ -232,13 +263,7 @@
     code = (cell_idx[:, 1] << Y_SHIFT) | (cell_idx[:, 0] << X_SHIFT) | cell_idx[:, 2]
     code = jnp.where(live_mask > 0, code, y_blk << Y_SHIFT).astype(F32)
     upper = cic_wts[:, :, 1]
-    return jnp.stack([code, charge, upper[:, 0], upper[:, 1], upper[:, 2]]).reshape(5, 128, LANES)
-
-
-def home_ranks():
-    a = lax.broadcasted_iota(jnp.int32, (128, LANES), 0)
-    b = lax.broadcasted_iota(jnp.int32, (128, LANES), 1)
-    return (a * 128 + (b & 7) * 16 + (b >> 3)).astype(F32)
+    return jnp.stack([code, charge, upper[:, 0], upper[:, 1], upper[:, 2]]).reshape(5, CHUNKS, LANES)
 
 
 def mul6(a, b):
@@ -336,7 +361,7 @@
         return out
 
 
-def x_kernel(plan, core_ref, rho_ref, gas_ref, mx_ref, own_ref, send_ref, tmp_ref):
+def x_kernel(plan, core_ref, rho_ref, gas_ref, far_ref, mx_ref, own_ref, send_ref, tmp_ref):
     step = pl.program_id(0)
     core = core_ref[0]
     n, kp = plan.n, plan.k_pad
@@ -346,29 +371,33 @@
         tmp_ref[...] = jnp.zeros(tmp_ref.shape, F32)
 
     live = (2 * step < plan.y_blk).astype(F32)
-    tmp_ref[:, :, :plan.z_blk] = gas_ref[...] * live
+    keep = live * core_ref[1].astype(F32)
+    tmp_ref[:, :, :plan.z_blk] = gas_ref[...] * keep + far_ref[...] * live
     data = jnp.concatenate([rho_ref[y, :n, :] + tmp_ref[y] for y in range(2)], axis=1)
     parts = split3(data)
-    for half, out in ((core, own_ref), (1 - core, send_ref)):
-        res = mul6([mx_ref[m, half] for m in range(3)], parts)
+    lhs = [jnp.concatenate([mx_ref[m, core], mx_ref[m, 1 - core]], axis=0) for m in range(3)]
+    res = mul6(lhs, parts)
+    for h, out in enumerate((own_ref, send_ref)):
         for y in range(2):
             for ri in range(2):
-                out[ri, y] = res[ri * kp:(ri + 1) * kp, y * LANES:(y + 1) * LANES]
-
-
-def x_call(plan, core, rho, gas, mx):
+                r0 = (2 * h + ri) * kp
+                out[ri, y] = res[r0:r0 + kp, y * LANES:(y + 1) * LANES]
+
+
+def x_call(plan, core, rho, gas, far, mx):
     steps = plan.y_even // 2
     last = plan.y_blk // 2 - 1
     shape = jax.ShapeDtypeStruct((2, plan.y_even, plan.k_pad, LANES), F32)
     out_spec = pl.BlockSpec((2, 2, plan.k_pad, LANES), lambda i: (0, i, 0, 0))
+    gas_spec = pl.BlockSpec((2, plan.n, plan.z_blk), lambda i: (jnp.minimum(i, last), 0, 0))
     return pl.pallas_call(
         functools.partial(x_kernel, plan), grid=(steps,), out_shape=(shape, shape),
         in_specs=[SMEM_SPEC, pl.BlockSpec((2, plan.x_pad, LANES), lambda i: (i, 0, 0)),
-                  pl.BlockSpec((2, plan.n, plan.z_blk), lambda i: (jnp.minimum(i, last), 0, 0)),
+                  gas_spec, gas_spec,
                   pl.BlockSpec(mx.shape, lambda i: (0, 0, 0, 0))],
         out_specs=(out_spec, out_spec),
         scratch_shapes=[pltpu.VMEM((2, plan.n, LANES), F32)], name="dft_x",
-    )(core, rho, gas, mx)
+    )(core, rho, gas, far, mx)
 
 
 Z_BATCH = 5
@@ -459,7 +488,9 @@
         energy = energy + weight * jnp.sum(power, axis=0, keepdims=True)
         parts = split3(jnp.concatenate([g_a * r0, g_a * r1, g_b * r2], axis=1))
         for i in range(plan.n_chip):
-            p = mul6([ei_ref[m, i] for m in range(3)], parts)
+            if i % 2 == 0:
+                two = mul6([ei_ref[m, i:i + 2].reshape(8 * yp, n) for m in range(3)], parts)
+            p = two[(i % 2) * 4 * yp:(i % 2 + 1) * 4 * yp]
             blk = [[p[u * yp:(u + 1) * yp, g * LANES:(g + 1) * LANES] for g in range(3)] for u in range(4)]
             co, si, ck, sk = blk
             pot = (co[0] - si[1], co[1] + si[0], co[2] - flip * pltpu.roll(si[2], 64, 1))
@@ -535,7 +566,7 @@
     )(core, rec, wi)
 
 
-def field_kernel(plan, n_blk, n_xt, e_norm, core_ref, table_ref, num_ref, slot_ref, own_ref, rec_ref, mi_ref,
+def field_kernel(plan, n_xt, e_norm, core_ref, table_ref, num_ref, slot_ref, own_ref, rec_ref, mi_ref,
                  out_ref, energy_ref, fhm_ref, flo_ref, lhs_ref):
     core = core_ref[0]
     kp = plan.k_pad
@@ -565,13 +596,13 @@
     lax.fori_loop(0, plan.y_even // 2, planes, 0)
     lanes = own_ref[0, 0, plan.y_even - 1, 0:1, :] + rec_ref[0, 0, plan.y_even - 1, 0:1, :]
     energy_ref[...] = jnp.broadcast_to(jnp.sum(lanes, axis=1, keepdims=True) * e_norm, energy_ref.shape)
-    interp_kernel(n_blk, n_xt, table_ref, num_ref, slot_ref, fhm_ref, flo_ref, out_ref)
-
-
-def field_call(plan, core, table, num, slots, own, rec, mi, n_blk, n_xt, e_norm):
-    return pl.pallas_call(
-        functools.partial(field_kernel, plan, n_blk, n_xt, e_norm),
-        out_shape=(jax.ShapeDtypeStruct((3, 128, LANES), F32), jax.ShapeDtypeStruct((8, LANES), F32)),
+    interp_kernel(n_xt, table_ref, num_ref, slot_ref, fhm_ref, flo_ref, out_ref)
+
+
+def field_call(plan, core, table, num, slots, own, rec, mi, n_xt, e_norm):
+    return pl.pallas_call(
+        functools.partial(field_kernel, plan, n_xt, e_norm),
+        out_shape=(jax.ShapeDtypeStruct((SLOT_ROWS, LANES), F32), jax.ShapeDtypeStruct((8, LANES), F32)),
         in_specs=[SMEM_SPEC, SMEM_SPEC, SMEM_SPEC] + [VMEM_SPEC] * 4, out_specs=(VMEM_SPEC, VMEM_SPEC),
         scratch_shapes=[pltpu.VMEM((plan.y_even, 3, plan.x_pad, 2 * LANES), BF16),
                         pltpu.VMEM((plan.y_even, 3, plan.x_pad, LANES), BF16),
@@ -586,7 +617,7 @@
     fine = jax.sharding.Mesh(mesh.devices.reshape(mesh.shape["rep"], n_cols, n_cx, 2), ("rep", "col", "cx", "core"))
     slot_axes = ("rep", "col", "cx", "core")
     chip_axes = ("cx", "col")
-    turn = [(a * 2 + b, b * 2 + a) for a in range(n_cols) for b in range(2)]
+    turn = [(a * 2 + b, b * 2 + a) for a in range(n_cols) for b in range(2) if a != b]
     other_core = [(0, 1), (1, 0)]
 
     def device_body(part_mass, cell_idx, cic_wts, live_mask, gas_block):
@@ -603,12 +634,19 @@
         n_xt = grid_size // X_TILE
         n_blk = y_blk * n_xt
 
-        raw = lax.ppermute(slot_arrays(part_mass, cell_idx, cic_wts, live_mask, y_blk), ("col", "core"), turn)
-        gas = lax.ppermute(jnp.transpose(gas_block, (1, 0, 2)), ("col", "core"), turn)
+        keep = (core == lax.axis_index("col")).astype(jnp.int32)
+
+        def swap(arr):
+            return lax.ppermute(arr, ("col", "core"), turn)
+
+        raw = slot_arrays(part_mass, cell_idx, cic_wts, live_mask, y_blk)
+        raw = swap(raw) + raw * keep.astype(F32)
+        raw, gas = lax.optimization_barrier((raw, jnp.transpose(gas_block, (1, 0, 2))))
+        gas_far = swap(gas)
         table, num = pair_table(raw[0].reshape(-1), n_blk, n_xt)
-        slots = sort_call(jnp.concatenate([raw, home_ranks()[None]]))
-        rho = deposit_call(table, num, slots, plan.y_even, grid_size, n_blk, n_xt)
-        own, send = x_call(plan, core_arr, rho, gas, tab["mx"])
+        slots = sort_call(raw)
+        rho = deposit_call(table, num, slots, plan.y_even, grid_size, n_xt)
+        own, send = x_call(plan, jnp.stack([core, keep]), rho, gas, gas_far, tab["mx"])
         rec = lax.ppermute(send, "core", other_core)
         to_y = z_call(plan, core_arr, own, rec, tab["wz"])
         at_y = lax.all_to_all(to_y, chip_axes, 0, 0, tiled=True)
@@ -617,9 +655,9 @@
         own, send = zi_call(plan, core_arr, at_z, tab["wi"])
         rec = lax.ppermute(send, "core", other_core)
         e_norm = 0.5 / (grid_size ** 3 * n_slots)
-        forces, energy = field_call(plan, core_arr, table, num, slots, own, rec, tab["mi"], n_blk, n_xt, e_norm)
-        back = sort_call(jnp.concatenate([slots[5:6], forces]))
-        home = lax.ppermute(back[1:4], ("col", "core"), turn)
+        forces, energy = field_call(plan, core_arr, table, num, slots, own, rec, tab["mi"], n_xt, e_norm)
+        back = unsort_call(slots, forces)
+        home = swap(back) + back * keep.astype(F32)
         return home.reshape(3, per_dev).T, energy[0, 0:1]
 
     return jax.shard_map(

time: 517 us -> 453 us (0.88)
  starting transfers between devices: 65.1 us -> 9.68 us
  Pallas kernels: 273 us -> 263 us
    ppermute x3, starting transfers between devices: 38.3 us -> 4.23 us  [swap(): return lax.ppermute(arr, ('col', 'core'), turn)]
    all_to_all x1, starting transfers between devices: 17.5 us -> 5.45 us  [device_body(): at_y = lax.all_to_all(to_y, chip_axes, 0, 0, tiled=True)]
    pallas_call x4, Pallas kernels: 164 us -> 153 us  [the longest x1 82.7 us: field_call(): pl.pallas_call(functools.partial(field_kernel, plan, n_xt, e_norm), out_s...]
    ppermute x2, starting transfers between devices: 9.32 us -> 0.01 us  [device_body(): rec = lax.ppermute(send, 'core', other_core)]
  transfers between devices with their start and end apart: 6 -> 6, of which waited for: 3 -> 3; matrix products, arithmetic and copies ran while one was open for 1% -> 3% of each run, Pallas kernels for 13% -> 13%
where the time goes in v3:
time: 453 us; the launch traced here: 452 us
  Pallas kernels  263 us (58%)
  blocking collectives  94.4 us (21%)
  waiting for transfers between devices  63.3 us (14%)
  local copies, waits for them, and re-layouts  12.7 us (3%)
  starting transfers between devices  9.68 us (2%)
  other arithmetic  8.29 us (2%)
    all_to_all x1, blocking collectives, device_body(): at_z = lax.all_to_all(from_y, chip_axes, 0, 0, tiled=True)  94.4 us
    pallas_call x1, Pallas kernels, field_call(): pl.pallas_call(functools.partial(field_kernel, plan, n_xt, e_norm), out_s...  82.7 us
    pallas_call x1, Pallas kernels, deposit_call(): pl.pallas_call(functools.partial(deposit_kernel, n_xt, grid_size), out_sh...  47.9 us
    all_to_all x1, waiting for transfers between devices, device_body(): at_y = lax.all_to_all(to_y, chip_axes, 0, 0, tiled=True)  44.7 us
    pallas_call x1, Pallas kernels, y_call(): pl.pallas_call(functools.partial(y_kernel, plan), out_shape=jax.ShapeDtyp...  38.2 us
    pallas_call x1, Pallas kernels, zi_call(): pl.pallas_call(functools.partial(zi_kernel, plan), grid=(plan.y_even // Z...  34.4 us
    pallas_call x1, Pallas kernels, x_call(): pl.pallas_call(functools.partial(x_kernel, plan), grid=(steps,), out_shap...  21.7 us
    ppermute x2, waiting for transfers between devices, device_body(): rec = lax.ppermute(send, 'core', other_core)  18.7 us
  transfers between devices with their start and end apart: 6, of which 3 were waited for; matrix products, arithmetic and copies ran while one was open for 3% of the time, Pallas kernels for 13%

profile of v3, /device:TPU:0, one launch (start us, length us, event | category | flops | bytes accessed | tf_op | source)
XLA Modules:
  0.0 451.8 jit_solution(15172850701040191085)
XLA Ops:
  0.6 1.3 slice_or_fusion
  1.9 1.2 slice.40
  3.1 0.1 copy.23
  3.3 0.1 fusion.7
  3.4 0.9 bitcast_dynamic-update-slice_fusion.1
  4.3 0.9 bitcast_dynamic-update-slice_fusion
  5.2 0.7 collective-permute-start
  5.9 6.0 %copy.21 = f32[192,48,96]{2,0,1:T(8,128)} copy(f32[192,48,96]{2,1,0:T(8,128)} %param.15) | data formatting | bytes 7077888 | tf_op args[4]
  12.0 0.0 collective-permute-done
  12.0 0.7 multiply_add_fusion.in_ref
  12.7 2.9 collective-permute-start.1
  15.6 0.7 pad_add_fusion.1.core_ref
  16.3 12.8 %slot_sort.1.slot_ref = f32[1032,128]{1,0:T(8,128)} custom-call(f32[5,128,128]{2,1,0:T(8,128)} %multiply_add_fusion.in_ref), custom_call_target="tpu_custom_call" | custom-call | tf_op jit(solution)/shard_map/slot_sort/pallas_call | solution.py:238
  29.0 0.8 slice_bitcast_fusion
  29.9 1.1 convert_reduce_fusion
  31.0 0.1 and_select_fusion
  31.0 0.1 select_reduce_fusion.2
  31.2 0.7 slice.47.num_ref
  31.8 0.1 convert_reduce_fusion.1
  31.9 0.1 fusion.8
  32.0 0.1 select_reduce_fusion.1
  32.1 0.7 fusion
  32.8 0.6 pad_add_fusion.table_ref
  33.4 47.9 %deposit.1.rho_ref = f32[50,208,128]{2,1,0:T(8,128)} custom-call(s32[3,224]{1,0:T(4,128)} %pad_add_fusion.table_ref, s32[1]{0:T(128)} %slice.47.num_ref, f32[1032,128]{1,0:T(8,128)} %slot_sort.1.slot_ref), custom_call_target="tpu_custom_call" | custom-call | tf_op jit(solution)/shard_map/deposit/pallas_call | solution.py:253
  81.3 0.0 collective-permute-done.1.far_ref
  81.3 21.7 %dft_x.1 = (f32[2,50,56,128]{3,2,1,0:T(8,128)}, f32[2,50,56,128]{3,2,1,0:T(8,128)}) custom-call(s32[2]{0:T(128)} %pad_add_fusion.1.core_ref, f32[50,208,128]{2,1,0:T(8,128)} %deposit.1.rho_ref, f32[48,192,96]{2,1,0:T(8,128)} %bitcast.28.gas_ref, f32[48,192,96]{2,1,0:T(8,128)} %collective-permute-done.1.far_ref, bf16[3,2,112,192]{3,2,1,0:T(8,128)(2,1)} %constant.85.clone.mx_ref), custom_call_target="tpu_custom_call" | custom-call | tf_op jit(solution)/shard_map/dft_x/pallas_call | solution.py:393
  103.0 0.0 collective-permute-start.2
  103.0 5.3 %collective-permute-done.2.rec_ref = f32[2,50,56,128]{3,2,1,0:T(8,128)S(1)} collective-permute-done((f32[2,50,56,128]{3,2,1,0:T(8,128)}, f32[2,50,56,128]{3,2,1,0:T(8,128)S(1)}, u32[]{:S(2)}, u32[]{:S(2)}) %collective-permute-start.2) | collective-permute-done | bytes 2867232 | tf_op jit(solution)/shard_map/ppermute | solution.py:650
  108.3 0.0 copy-start
  108.3 1.6 copy-done
  109.9 14.9 %dft_z.1 = f32[4,3,640,128]{3,2,1,0:T(8,128)} custom-call(s32[1]{0:T(128)} %bitcast.7.core_ref, f32[2,50,56,128]{3,2,1,0:T(8,128)} %get-tuple-element.12.own_ref, f32[2,50,56,128]{3,2,1,0:T(8,128)} %copy-done, bf16[3,2,2,128,384]{4,3,2,1,0:T(8,128)(2,1)} %constant.86.clone.wz_ref), custom_call_target="tpu_custom_call" | custom-call | tf_op jit(solution)/shard_map/dft_z/pallas_call | solution.py:437
  124.8 5.5 %all-to-all-start = ((f32[4,3,640,128]{3,2,1,0:T(8,128)}), f32[4,3,640,128]{3,2,1,0:T(8,128)}, u32[]{:S(2)}, u32[]{:S(2)}) async-start(f32[4,3,640,128]{3,2,1,0:T(8,128)} %dft_z.1), calls=%async_computation | async-start | bytes 7864320 | tf_op jit(solution)/shard_map/all_to_all | solution.py:652
  130.3 44.7 %all-to-all-done.rec_ref = f32[4,3,640,128]{3,2,1,0:T(8,128)} async-done(((f32[4,3,640,128]{3,2,1,0:T(8,128)}), f32[4,3,640,128]{3,2,1,0:T(8,128)}, u32[]{:S(2)}, u32[]{:S(2)}) %all-to-all-start) | async-done | bytes 3932192 | tf_op jit(solution)/shard_map/all_to_all | solution.py:652
  174.9 38.2 %dft_y.1 = f32[4,2,3,640,128]{4,3,2,1,0:T(8,128)} custom-call(s32[1]{0:T(128)} %bitcast.13.base_ref, f32[4,3,640,128]{3,2,1,0:T(8,128)} %all-to-all-done.rec_ref, bf16[3,384,224]{2,1,0:T(8,128)(2,1)} %constant.87.clone.my_ref, bf16[3,4,224,192]{3,2,1,0:T(8,128)(2,1)} %constant.88.clone.ei_ref), custom_call_target="tpu_custom_call" | custom-call | tf_op jit(solution)/shard_map/dft_y/pallas_call | solution.py:510
  213.1 94.4 %all_to_all.10.rec_ref = f32[4,2,3,640,128]{4,3,2,1,0:T(8,128)} all-to-all(f32[4,2,3,640,128]{4,3,2,1,0:T(8,128)} %dft_y.1), channel_id=1, replica_groups=mesh['rep'=1,'col'=2,'cx'=2,'core'=2] {'cx','col'}, dimensions={0} | all-to-all | bytes 15728640 | tf_op jit(solution)/shard_map/all_to_all | solution.py:654
  307.5 34.4 %idft_z.1 = (f32[3,2,50,56,128]{4,3,2,1,0:T(8,128)}, f32[3,2,50,56,128]{4,3,2,1,0:T(8,128)}) custom-call(s32[1]{0:T(128)} %bitcast.7.core_ref, f32[4,2,3,640,128]{4,3,2,1,0:T(8,128)} %all_to_all.10.rec_ref, bf16[3,2,384,512]{3,2,1,0:T(8,128)(2,1)} %constant.89.clone.wi_ref), custom_call_target="tpu_custom_call" | custom-call | tf_op jit(solution)/shard_map/idft_z/pallas_call | solution.py:560
  341.9 0.0 collective-permute-start.3
  341.9 13.4 %collective-permute-done.3.rec_ref = f32[3,2,50,56,128]{4,3,2,1,0:T(8,128)} collective-permute-done((f32[3,2,50,56,128]{4,3,2,1,0:T(8,128)}, f32[3,2,50,56,128]{4,3,2,1,0:T(8,128)}, u32[]{:S(2)}, u32[]{:S(2)}) %collective-permute-start.3) | collective-permute-done | bytes 8601632 | tf_op jit(solution)/shard_map/ppermute | solution.py:656
  355.3 82.7 %idft_x_interp.1 = (f32[1032,128]{1,0:T(8,128)}, f32[8,128]{1,0:T(8,128)}) custom-call(s32[1]{0:T(128)} %bitcast.7.core_ref, s32[3,224]{1,0:T(4,128)} %pad_add_fusion.table_ref, s32[1]{0:T(128)} %slice.47.num_ref, f32[1032,128]{1,0:T(8,128)} %slot_sort.1.slot_ref, f32[3,2,50,56,128]{4,3,2,1,0:T(8,128)} %get-tuple-element.14.own_ref, ...), custom_call_target="tpu_custom_call" | custom-call | tf_op jit(solution)/shard_map/idft_x_interp/pallas_call | solution.py:603
  438.0 10.1 %slot_unsort.1 = f32[3,128,128]{2,1,0:T(8,128)} custom-call(f32[1032,128]{1,0:T(8,128)} %slot_sort.1.slot_ref, f32[1032,128]{1,0:T(8,128)} %get-tuple-element.16.force_ref), custom_call_target="tpu_custom_call" | custom-call | tf_op jit(solution)/shard_map/slot_unsort/pallas_call | solution.py:245
  448.1 0.7 collective-permute-start.4
  448.8 1.2 slice.48
  450.0 0.0 collective-permute-done.4
  450.0 1.0 add_bitcast_fusion
  450.9 0.8 copy.22
  (4 shorter events, 0.0 us)
Async XLA Ops:
  5.2 6.7 %collective-permute-start = (f32[5,128,128]{2,1,0:T(8,128)S(1)}, f32[5,128,128]{2,1,0:T(8,128)S(1)}, u32[]{:S(2)}, u32[]{:S(2)}) collective-permute-start(f32[5,128,128]{2,1,0:T(8,128)S(1)} %constant_dynamic-update-slice_fusion), channel_id=1, source_target_pairs={{1,4},{4,1},{3,6},{6,3}} | collective-permute-start | bytes 983048 | tf_op jit(solution)/shard_map/ppermute | solution.py:640
  12.7 68.6 %collective-permute-start.1 = (f32[48,192,96]{2,1,0:T(8,128)}, f32[48,192,96]{2,1,0:T(8,128)}, u32[]{:S(2)}, u32[]{:S(2)}) collective-permute-start(f32[48,192,96]{2,1,0:T(8,128)} %bitcast.28.gas_ref), channel_id=1, source_target_pairs={{1,4},{4,1},{3,6},{6,3}} | collective-permute-start | bytes 10616840 | tf_op jit(solution)/shard_map/ppermute | solution.py:640
  103.0 5.3 %collective-permute-start.2 = (f32[2,50,56,128]{3,2,1,0:T(8,128)}, f32[2,50,56,128]{3,2,1,0:T(8,128)S(1)}, u32[]{:S(2)}, u32[]{:S(2)}) collective-permute-start(f32[2,50,56,128]{3,2,1,0:T(8,128)} %get-tuple-element.13), channel_id=1, source_target_pairs={{0,1},{1,0},{2,3},{3,2},{4,5},{5,4},{6,7},{7,6}} | collective-permute-start | bytes 8601608 | tf_op jit(solution)/shard_map/ppermute | solution.py:650
  108.3 1.6 copy-start
  124.8 50.1 %all-to-all-start = ((f32[4,3,640,128]{3,2,1,0:T(8,128)}), f32[4,3,640,128]{3,2,1,0:T(8,128)}, u32[]{:S(2)}, u32[]{:S(2)}) async-start(f32[4,3,640,128]{3,2,1,0:T(8,128)} %dft_z.1), calls=%async_computation | async-start | bytes 7864320 | tf_op jit(solution)/shard_map/all_to_all | solution.py:652
  341.9 13.4 %collective-permute-start.3 = (f32[3,2,50,56,128]{4,3,2,1,0:T(8,128)}, f32[3,2,50,56,128]{4,3,2,1,0:T(8,128)}, u32[]{:S(2)}, u32[]{:S(2)}) collective-permute-start(f32[3,2,50,56,128]{4,3,2,1,0:T(8,128)} %get-tuple-element.15), channel_id=1, source_target_pairs={{0,1},{1,0},{2,3},{3,2},{4,5},{5,4},{6,7},{7,6}} | collective-permute-start | bytes 25804808 | tf_op jit(solution)/shard_map/ppermute | solution.py:656
  448.1 1.9 collective-permute-start.4
